TPU v7x, 8 devices: a whole 2x2x1 slice. The times are simulated.
8 devices in a mesh: rep: 2 (over z, y), fsdp: 4 (over x, core).
Axes of the slice: x: 2, y: 2, z: 1, core: 2. Of those that a mesh axis runs over, the one named last changes fastest.
Arguments:
- tokens: bfloat16 [8192, 2048], P(('rep', 'fsdp')), parts along dimension 0
- seg_ids: int32 [8192], P(('rep', 'fsdp')), parts along dimension 0
- w_q: bfloat16 [2, 2048, 2048], P(None, 'fsdp')
- w_k: bfloat16 [2, 2048, 256], P(None, 'fsdp')
- w_v: bfloat16 [2, 2048, 256], P(None, 'fsdp')
- w_o: bfloat16 [2, 2048, 2048], P(None, 'fsdp')
- w_gate: bfloat16 [2, 2048, 11008], P(None, 'fsdp')
- w_up: bfloat16 [2, 2048, 11008], P(None, 'fsdp')
- w_down: bfloat16 [2, 11008, 2048], P(None, 'fsdp')
- g_attn: bfloat16 [2, 2048], replicated
- g_mlp: bfloat16 [2, 2048], replicated
Outputs:
- output: float32 [8192, 2048], P(('rep', 'fsdp')), parts along dimension 0
There are 2 independent parts. A program takes and returns all parts, laid end to end along the dimension named above; an argument that names none is the same for every part.
All inputs are finite; a program needn't handle non-finite values.
Results may differ from a plain program's by a relative error of at most 0.0135712.
Values are sent between devices in bfloat16 or wider.
A program may use at most 1 GiB of HBM per device.

v0:
```python
import jax
import jax.numpy as jnp
from jax import lax
from jax.sharding import PartitionSpec as P

HEAD = 128
EPS = 1e-5
ROPE_BASE = 10000.0


def rms_norm(hidden, gain):
    inv_rms = lax.rsqrt(jnp.mean(hidden * hidden, axis=-1, keepdims=True) + EPS)
    return (hidden * inv_rms * gain.astype(jnp.float32)).astype(jnp.bfloat16)


def rope_tables(seg_blk):
    tok_idx = lax.broadcasted_iota(jnp.int32, seg_blk.shape, 1)
    is_first = jnp.concatenate([tok_idx[:, :1] == 0, seg_blk[:, 1:] != seg_blk[:, :-1]], axis=1)
    req_start = lax.cummax(jnp.where(is_first, tok_idx, 0), axis=1)
    tok_pos = (tok_idx - req_start).astype(jnp.float32)
    half_dim = HEAD // 2
    inv_freq = ROPE_BASE ** (-jnp.arange(half_dim, dtype=jnp.float32) / half_dim)
    angles = tok_pos[:, :, None] * inv_freq
    return jnp.cos(angles), jnp.sin(angles)


def attention_mask(seg_blk):
    tok_idx = jnp.arange(seg_blk.shape[1], dtype=jnp.int32)
    causal = tok_idx[:, None] >= tok_idx[None, :]
    same_req = seg_blk[:, :, None] == seg_blk[:, None, :]
    return (same_req & causal)[:, None, None]


def apply_rope(vals, cos_tab, sin_tab):
    half_dim = HEAD // 2
    bcast_shape = cos_tab.shape[:2] + (1,) * (vals.ndim - 3) + (half_dim,)
    cos_wide = cos_tab.reshape(bcast_shape)
    sin_wide = sin_tab.reshape(bcast_shape)
    first_half = vals[..., :half_dim].astype(jnp.float32)
    second_half = vals[..., half_dim:].astype(jnp.float32)
    rotated = jnp.concatenate([first_half * cos_wide - second_half * sin_wide, second_half * cos_wide + first_half * sin_wide], axis=-1)
    return rotated.astype(jnp.bfloat16)


def attend(q_proj, k_proj, v_proj, allowed, cos_tab, sin_tab):
    n_blk = q_proj.shape[0]
    n_tok = q_proj.shape[1]
    kv_heads = k_proj.shape[2] // HEAD
    group_size = q_proj.shape[2] // k_proj.shape[2]
    q_rot = apply_rope(q_proj.reshape(n_blk, n_tok, kv_heads, group_size, HEAD), cos_tab, sin_tab)
    k_rot = apply_rope(k_proj.reshape(n_blk, n_tok, kv_heads, HEAD), cos_tab, sin_tab)
    v_heads = v_proj.reshape(n_blk, n_tok, kv_heads, HEAD)
    scores = jnp.einsum("btkgd,bskd->bkgts", q_rot, k_rot, preferred_element_type=jnp.float32) * HEAD ** -0.5
    scores = jnp.where(allowed, scores, -1e30)
    probs = jax.nn.softmax(scores, axis=-1).astype(jnp.bfloat16)
    mixed = jnp.einsum("bkgts,bskd->btkgd", probs, v_heads, preferred_element_type=jnp.float32)
    return mixed.astype(jnp.bfloat16).reshape(n_blk, n_tok, q_proj.shape[2])


def decoder_layer(hidden, allowed, cos_tab, sin_tab, w_q, w_k, w_v, w_o, w_gate, w_up, w_down, g_attn, g_mlp):
    normed = rms_norm(hidden, g_attn)
    q_proj = jnp.dot(normed, w_q, preferred_element_type=jnp.float32).astype(jnp.bfloat16)
    k_proj = jnp.dot(normed, w_k, preferred_element_type=jnp.float32).astype(jnp.bfloat16)
    v_proj = jnp.dot(normed, w_v, preferred_element_type=jnp.float32).astype(jnp.bfloat16)
    mixed = attend(q_proj, k_proj, v_proj, allowed, cos_tab, sin_tab)
    hidden = hidden + jnp.dot(mixed, w_o, preferred_element_type=jnp.float32)
    normed = rms_norm(hidden, g_mlp)
    gate_proj = jnp.dot(normed, w_gate, preferred_element_type=jnp.float32)
    up_proj = jnp.dot(normed, w_up, preferred_element_type=jnp.float32)
    act_val = (jax.nn.silu(gate_proj) * up_proj).astype(jnp.bfloat16)
    return hidden + jnp.dot(act_val, w_down, preferred_element_type=jnp.float32)


def gather_rows(w_shard):
    return lax.all_gather(w_shard, "fsdp", axis=0, tiled=True)


def solution(mesh):
    tok_spec = P(("rep", "fsdp"), None)
    seg_spec = P(("rep", "fsdp"))
    mat_spec = P(None, "fsdp", None)
    gain_spec = P(None, None)

    def per_device(tokens, seg_ids, w_q, w_k, w_v, w_o, w_gate, w_up, w_down, g_attn, g_mlp):
        n_tok, width = tokens.shape
        seg_blk = seg_ids.reshape(1, n_tok)
        cos_tab, sin_tab = rope_tables(seg_blk)
        allowed = attention_mask(seg_blk)
        hidden = tokens.astype(jnp.float32).reshape(1, n_tok, width)
        for layer in range(w_q.shape[0]):
            full_q = gather_rows(w_q[layer])
            full_k = gather_rows(w_k[layer])
            full_v = gather_rows(w_v[layer])
            full_o = gather_rows(w_o[layer])
            full_gate = gather_rows(w_gate[layer])
            full_up = gather_rows(w_up[layer])
            full_down = gather_rows(w_down[layer])
            hidden = decoder_layer(hidden, allowed, cos_tab, sin_tab, full_q, full_k, full_v, full_o, full_gate, full_up, full_down, g_attn[layer], g_mlp[layer])
        return hidden.reshape(n_tok, width)

    return jax.shard_map(per_device, mesh=mesh, in_specs=(tok_spec, seg_spec, mat_spec, mat_spec, mat_spec, mat_spec, mat_spec, mat_spec, mat_spec, gain_spec, gain_spec), out_specs=tok_spec, check_vma=False)
```

profile of v0, /device:TPU:0, one launch (start us, length us, event | category | flops | bytes accessed | tf_op | source)
XLA Modules:
  0.0 1968.2 jit_solution(7727448192732094503)
XLA Ops:
  20.2 15.7 fusion.116
  35.9 15.7 fusion.115
  51.7 16.1 fusion.117
  117.3 24.1 %fusion.2 = (f32[2,8,1024]{2,1,0:T(8,128)S(1)}, f32[2,1024,1024,8]{2,1,3,0:T(8,128)}) fusion(pred[1024,1024]{0,1:T(8,128)(4,1)S(1)} %fusion.58, bf16[1024,2,8,64]{3,0,2,1:T(8,128)(2,1)S(1)} %get-tuple-element.14, bf16[1024,2,8,64]{3,0,2,1:T(8,128)(2,1)S(1)} %get-tuple-element.13, bf16[1024,2,64]{2,0,1:T(8,128)(2,1)S(1)} %get-tuple-element.26, ...), kind=kOutput, calls=%fused_computation.8 | convolution fusion | flops 4354719744 | bytes 72941568 | tf_op jit(solution)/shard_map/btkgd,bskd->bkgts/dot_general | solution.py:53
  141.4 21.6 %fusion = f32[2,8,1024]{2,1,0:T(8,128)S(1)} fusion(f32[2,1024,1024,8]{2,1,3,0:T(8,128)} %get-tuple-element.42, f32[2,8,1024]{2,1,0:T(8,128)S(1)} %get-tuple-element.41, pred[1024,1024]{0,1:T(8,128)(4,1)S(1)} %fusion.58), kind=kLoop, calls=%fused_computation.6 | loop fusion | flops 67092480 | bytes 68288512 | tf_op jit(solution)/shard_map/reduce_sum | solution.py:55
  163.0 28.0 %fusion.76 = bf16[2,128,8,1024]{3,1,2,0:T(8,128)(2,1)} fusion(bf16[1024,2,128,1]{0,2,3,1:T(8,128)(2,1)S(1)} %bitcast.219, f32[2,8,1024]{2,1,0:T(8,128)S(1)} %fusion, f32[2,8,1024]{2,1,0:T(8,128)S(1)} %get-tuple-element.41, f32[2,1024,1024,8]{2,1,3,0:T(8,128)} %get-tuple-element.42, pred[1024,1024]{0,1:T(8,128)(4,1)S(1)} %fusion.58), kind=kOutput, calls=%fused_computation.83 | convolution fusion | flops 4380950528 | bytes 73007104 | tf_op jit(solution)/shard_map/bkgts,bskd->btkgd/dot_general | solution.py:56
  191.0 15.7 multiply_reduce_fusion.2
  206.7 215.3 %all-gather.37.cloned.1.call-done = bf16[1,2048,11008]{2,1,0:T(8,128)(2,1)} async-done(((bf16[1,512,11008]{2,1,0:T(8,128)(2,1)}), bf16[1,2048,11008]{2,1,0:T(8,128)(2,1)}) %all-gather.37.cloned.1.call-update) | async-done | bytes 45088784 | tf_op jit(solution)/shard_map/all_gather | solution.py:75
  422.0 56.4 %fusion.14 = f32[1024,11008]{1,0:T(8,128)} fusion(bf16[1,2048,11008]{2,1,0:T(8,128)(2,1)} %all-gather.37.cloned.1.call-done, f32[1024,2048]{1,0:T(8,128)} %get-tuple-element.44, f32[2048]{0:T(1024)S(1)} %bitcast.211, f32[1024]{0:T(1024)S(1)} %add_rsqrt_fusion.2), kind=kOutput, calls=%fused_computation.20 | convolution fusion | flops 46177189888 | bytes 98578432 | tf_op jit(solution)/shard_map/dot_general | solution.py:68
  478.4 210.4 %all-gather.39.cloned.1.call-done = bf16[1,2048,11008]{2,1,0:T(8,128)(2,1)} async-done(((bf16[1,512,11008]{2,1,0:T(8,128)(2,1)}), bf16[1,2048,11008]{2,1,0:T(8,128)(2,1)}) %all-gather.39.cloned.1.call-update) | async-done | bytes 45088784 | tf_op jit(solution)/shard_map/all_gather | solution.py:75
  688.8 65.1 %multiply_convert_fusion.1.clone.1.clone.4 = bf16[1024,11008]{1,0:T(8,128)(2,1)} fusion(f32[1024,11008]{1,0:T(8,128)} %fusion.14, bf16[1,2048,11008]{2,1,0:T(8,128)(2,1)} %all-gather.39.cloned.1.call-done, f32[1024,2048]{1,0:T(8,128)} %get-tuple-element.44, f32[2048]{0:T(1024)S(1)} %bitcast.212, f32[1024]{0:T(1024)S(1)} %add_rsqrt_fusion.2), kind=kOutput, calls=%fused_computation.23.clone.clone.clone.clone.clone.1 | convolution fusion | flops 46244823040 | bytes 121122816 | tf_op jit(solution)/shard_map/dot_general | solution.py:69
  753.9 201.9 %all-gather.41.cloned.1.call-done = bf16[1,11008,2048]{2,1,0:T(8,128)(2,1)} async-done(((bf16[1,2752,2048]{2,1,0:T(8,128)(2,1)}), bf16[1,11008,2048]{2,1,0:T(8,128)(2,1)}) %all-gather.41.cloned.1.call-update) | async-done | bytes 45088784 | tf_op jit(solution)/shard_map/all_gather | solution.py:75
  955.8 60.1 %multiply_reduce_fusion.1 = (f32[1024]{0:T(1024)S(1)}, f32[1024,2048]{1,0:T(8,128)}) fusion(f32[1024,2048]{1,0:T(8,128)} %get-tuple-element.44, bf16[1,11008,2048]{2,1,0:T(8,128)(2,1)} %all-gather.41.cloned.1.call-done, bf16[1024,11008]{1,0:T(8,128)(2,1)} %multiply_convert_fusion.1.clone.1.clone.4), kind=kOutput, calls=%fused_computation.61 | convolution fusion | flops 46177189888 | bytes 84414464 | tf_op jit(solution)/shard_map/dot_general | solution.py:71
  1028.4 13.9 fusion.73
  1071.8 24.3 %fusion.3 = (f32[2,8,1024]{2,1,0:T(8,128)S(1)}, f32[2,1024,1024,8]{2,1,3,0:T(8,128)}) fusion(pred[1024,1024]{0,1:T(8,128)(4,1)S(1)} %copy-done.1, bf16[1024,2,8,64]{3,0,2,1:T(8,128)(2,1)S(1)} %get-tuple-element.12, bf16[1024,2,8,64]{3,0,2,1:T(8,128)(2,1)S(1)} %get-tuple-element.11, bf16[1024,2,64]{2,0,1:T(8,128)(2,1)S(1)} %get-tuple-element.24, ...), kind=kOutput, calls=%fused_computation.9 | convolution fusion | flops 4354719744 | bytes 72941568 | tf_op jit(solution)/shard_map/btkgd,bskd->bkgts/dot_general | solution.py:53
  1096.1 21.6 %fusion.1 = f32[2,8,1024]{2,1,0:T(8,128)S(1)} fusion(f32[2,1024,1024,8]{2,1,3,0:T(8,128)} %get-tuple-element.48, f32[2,8,1024]{2,1,0:T(8,128)S(1)} %get-tuple-element.47, pred[1024,1024]{0,1:T(8,128)(4,1)S(1)} %copy-done.1), kind=kLoop, calls=%fused_computation.7 | loop fusion | flops 67092480 | bytes 68288512 | tf_op jit(solution)/shard_map/reduce_sum | solution.py:55
  1117.7 27.7 %fusion.79 = bf16[2,128,8,1024]{3,1,2,0:T(8,128)(2,1)} fusion(bf16[1024,2,128,1]{0,2,3,1:T(8,128)(2,1)S(1)} %bitcast.220, f32[2,8,1024]{2,1,0:T(8,128)S(1)} %fusion.1, f32[2,8,1024]{2,1,0:T(8,128)S(1)} %get-tuple-element.47, f32[2,1024,1024,8]{2,1,3,0:T(8,128)} %get-tuple-element.48, pred[1024,1024]{0,1:T(8,128)(4,1)S(1)} %copy-done.1), kind=kOutput, calls=%fused_computation.84 | convolution fusion | flops 4380950528 | bytes 73007104 | tf_op jit(solution)/shard_map/bkgts,bskd->btkgd/dot_general | solution.py:56
  1145.4 16.3 multiply_reduce_fusion
  1161.8 205.9 %all-gather.51.cloned.1.call-done = bf16[1,2048,11008]{2,1,0:T(8,128)(2,1)} async-done(((bf16[1,512,11008]{2,1,0:T(8,128)(2,1)}), bf16[1,2048,11008]{2,1,0:T(8,128)(2,1)}) %all-gather.51.cloned.1.call-update) | async-done | bytes 45088784 | tf_op jit(solution)/shard_map/all_gather | solution.py:75
  1367.7 56.4 %fusion.8 = f32[1024,11008]{1,0:T(8,128)} fusion(bf16[1,2048,11008]{2,1,0:T(8,128)(2,1)} %all-gather.51.cloned.1.call-done, f32[1024,2048]{1,0:T(8,128)} %get-tuple-element.50, f32[2048]{0:T(1024)S(1)} %bitcast.209, f32[1024]{0:T(1024)S(1)} %add_rsqrt_fusion), kind=kOutput, calls=%fused_computation.14 | convolution fusion | flops 46177189888 | bytes 98578432 | tf_op jit(solution)/shard_map/dot_general | solution.py:68
  1424.1 210.6 %all-gather.53.cloned.1.call-done = bf16[1,2048,11008]{2,1,0:T(8,128)(2,1)} async-done(((bf16[1,512,11008]{2,1,0:T(8,128)(2,1)}), bf16[1,2048,11008]{2,1,0:T(8,128)(2,1)}) %all-gather.53.cloned.1.call-update) | async-done | bytes 45088784 | tf_op jit(solution)/shard_map/all_gather | solution.py:75
  1634.6 65.2 %multiply_convert_fusion.clone.4 = bf16[1024,11008]{1,0:T(8,128)(2,1)} fusion(f32[1024,11008]{1,0:T(8,128)} %fusion.8, bf16[1,2048,11008]{2,1,0:T(8,128)(2,1)} %all-gather.53.cloned.1.call-done, f32[1024,2048]{1,0:T(8,128)} %get-tuple-element.50, f32[2048]{0:T(1024)S(1)} %bitcast.210, f32[1024]{0:T(1024)S(1)} %add_rsqrt_fusion), kind=kOutput, calls=%fused_computation.22.clone.clone.clone.1 | convolution fusion | flops 46244823040 | bytes 121122816 | tf_op jit(solution)/shard_map/dot_general | solution.py:69
  1699.8 201.6 %all-gather.55.cloned.1.call-done = bf16[1,11008,2048]{2,1,0:T(8,128)(2,1)} async-done(((bf16[1,2752,2048]{2,1,0:T(8,128)(2,1)}), bf16[1,11008,2048]{2,1,0:T(8,128)(2,1)}) %all-gather.55.cloned.1.call-update) | async-done | bytes 45088784 | tf_op jit(solution)/shard_map/all_gather | solution.py:75
  1901.5 59.7 %fusion.66 = f32[1024,2048]{1,0:T(8,128)} fusion(f32[1024,2048]{1,0:T(8,128)} %get-tuple-element.50, bf16[1,11008,2048]{2,1,0:T(8,128)(2,1)} %all-gather.55.cloned.1.call-done, bf16[1024,11008]{1,0:T(8,128)(2,1)} %multiply_convert_fusion.clone.4), kind=kOutput, calls=%fused_computation.81 | convolution fusion | flops 46172995584 | bytes 84410368 | tf_op jit(solution)/shard_map/dot_general | solution.py:71
  (114 shorter events, 104.8 us)
Async XLA Ops:
  6.5 74.0 %all-gather.31.cloned.1.call-start = ((), (), s32[]{:S(2)}) async-start(), calls=%async_computation.1 | async-start | bytes 1310720 | tf_op jit(solution)/shard_map/all_gather | solution.py:75
  8.4 80.1 %all-gather.29.cloned.1.call-start = ((), (), s32[]{:S(2)}) async-start(), calls=%async_computation | async-start | bytes 1310720 | tf_op jit(solution)/shard_map/all_gather | solution.py:75
  10.4 87.6 %all-gather.33.cloned.1.call-start = ((), (), s32[]{:S(2)}) async-start(), calls=%async_computation.2 | async-start | bytes 10485760 | tf_op jit(solution)/shard_map/all_gather | solution.py:75
  15.3 175.7 %all-gather.35.cloned.1.call-start = ((), (), s32[]{:S(2)}) async-start(), calls=%async_computation.3 | async-start | bytes 10485760 | tf_op jit(solution)/shard_map/all_gather | solution.py:75
  20.2 401.8 %all-gather.37.cloned.1.call-start = ((), (), s32[]{:S(2)}) async-start(), calls=%async_computation.4 | async-start | bytes 56360960 | tf_op jit(solution)/shard_map/all_gather | solution.py:75
  35.9 652.9 %all-gather.39.cloned.1.call-start = ((), (), s32[]{:S(2)}) async-start(), calls=%async_computation.5 | async-start | bytes 56360960 | tf_op jit(solution)/shard_map/all_gather | solution.py:75
  51.7 904.1 %all-gather.41.cloned.1.call-start = ((), (), s32[]{:S(2)}) async-start(), calls=%async_computation.6 | async-start | bytes 56360960 | tf_op jit(solution)/shard_map/all_gather | solution.py:75
  67.9 954.1 %all-gather.45.cloned.1.call-start = ((), (), s32[]{:S(2)}) async-start(), calls=%async_computation.8 | async-start | bytes 1310720 | tf_op jit(solution)/shard_map/all_gather | solution.py:75
  68.7 959.7 %all-gather.47.cloned.1.call-start = ((), (), s32[]{:S(2)}) async-start(), calls=%async_computation.9 | async-start | bytes 10485760 | tf_op jit(solution)/shard_map/all_gather | solution.py:75
  69.4 994.3 %all-gather.43.cloned.1.call-start = ((), (), s32[]{:S(2)}) async-start(), calls=%async_computation.7 | async-start | bytes 1310720 | tf_op jit(solution)/shard_map/all_gather | solution.py:75
  70.0 1075.4 %all-gather.49.cloned.1.call-start = ((), (), s32[]{:S(2)}) async-start(), calls=%async_computation.10 | async-start | bytes 10485760 | tf_op jit(solution)/shard_map/all_gather | solution.py:75
  70.7 1296.9 %all-gather.51.cloned.1.call-start = ((), (), s32[]{:S(2)}) async-start(), calls=%async_computation.11 | async-start | bytes 56360960 | tf_op jit(solution)/shard_map/all_gather | solution.py:75
  71.3 1563.3 %all-gather.53.cloned.1.call-start = ((), (), s32[]{:S(2)}) async-start(), calls=%async_computation.12 | async-start | bytes 56360960 | tf_op jit(solution)/shard_map/all_gather | solution.py:75
  72.1 1829.4 %all-gather.55.cloned.1.call-start = ((), (), s32[]{:S(2)}) async-start(), calls=%async_computation.13 | async-start | bytes 56360960 | tf_op jit(solution)/shard_map/all_gather | solution.py:75
  77.0 86.0 %copy-start = (pred[1024,1024]{0,1:T(8,128)(4,1)}, pred[1024,1024]{0,1:T(8,128)(4,1)S(1)}, u32[]{:S(2)}) copy-start(pred[1024,1024]{0,1:T(8,128)(4,1)S(1)} %fusion.58) | copy-start | bytes 3145732
  80.5 33.6 %copy-start.4 = (f32[1024,64]{1,0:T(8,128)}, f32[1024,64]{1,0:T(8,128)S(1)}, u32[]{:S(2)}) copy-start(f32[1024,64]{1,0:T(8,128)S(1)} %get-tuple-element.39) | copy-start | bytes 786436
  80.5 33.6 %copy-start.6 = (f32[1024,64]{1,0:T(8,128)}, f32[1024,64]{1,0:T(8,128)S(1)}, u32[]{:S(2)}) copy-start(f32[1024,64]{1,0:T(8,128)S(1)} %get-tuple-element.40) | copy-start | bytes 786436
  141.4 21.6 %copy-start.14 = (bf16[1024,256]{0,1:T(8,128)(2,1)S(1)}, bf16[1024,256]{0,1:T(8,128)(2,1)}, u32[]{:S(2)}) copy-start(bf16[1024,256]{0,1:T(8,128)(2,1)} %convolution_convert_fusion.3) | copy-start | bytes 1572868
  191.0 231.0 %copy-start.13 = (f32[1,2048]{1,0:T(1,128)S(1)}, f32[1,2048]{1,0:T(1,128)}, u32[]{:S(2)}) copy-start(f32[1,2048]{1,0:T(1,128)} %get-tuple-element.36) | copy-start | bytes 24580
  753.9 262.0 %copy-start.9 = (f32[1,2048]{1,0:T(1,128)S(1)}, f32[1,2048]{1,0:T(1,128)}, u32[]{:S(2)}) copy-start(f32[1,2048]{1,0:T(1,128)} %get-tuple-element.37) | copy-start | bytes 24580
  1053.6 9.7 copy-start.5
  1053.7 9.7 copy-start.7
  1096.1 21.6 %copy-start.15 = (bf16[1024,256]{0,1:T(8,128)(2,1)S(1)}, bf16[1024,256]{0,1:T(8,128)(2,1)}, u32[]{:S(2)}) copy-start(bf16[1024,256]{0,1:T(8,128)(2,1)} %convolution_convert_fusion.1) | copy-start | bytes 1572868
  1145.4 222.2 %copy-start.12 = (f32[1,2048]{1,0:T(1,128)S(1)}, f32[1,2048]{1,0:T(1,128)}, u32[]{:S(2)}) copy-start(f32[1,2048]{1,0:T(1,128)} %get-tuple-element.35) | copy-start | bytes 24580
  (6 other events, 23.8 us)
Sparse Core Ops, SparseCore 0:
  8.9 16.5 all-gather.30
  27.0 13.7 all-gather.28
  42.2 55.7 all-gather.32
  99.4 55.7 all-gather.34
  156.5 265.4 all-gather.36
  423.4 265.4 all-gather.38
  690.4 265.4 all-gather.40
  957.3 13.7 all-gather.44
  972.6 55.7 all-gather.46
  1029.8 13.7 all-gather.42
  1045.0 55.7 all-gather.48
  1102.2 265.4 all-gather.50
  1369.2 265.4 all-gather.52
  1636.0 265.4 all-gather.54
where the time goes:
time: 1980 us; the launch traced here: 1970 us
  waiting for transfers between devices  1260 us (64%)
  matrix products  543 us (27%)
  local copies, waits for them, and re-layouts  88.8 us (4%)
  other arithmetic  64.7 us (3%)
    all_gather x14, waiting for transfers between devices, gather_rows(): return lax.all_gather(w_shard, 'fsdp', axis=0, tiled=True)  1250 us
    dot_general x2, matrix products, decoder_layer(): up_proj = jnp.dot(normed, w_up, preferred_element_type=jnp.float32)  130 us
    dot_general x2, matrix products, decoder_layer(): return hidden + jnp.dot(act_val, w_down, preferred_element_type=jnp.float32)  120 us
    dot_general x2, matrix products, decoder_layer(): gate_proj = jnp.dot(normed, w_gate, preferred_element_type=jnp.float32)  113 us
    dot_general x2, matrix products, attend(): jnp.einsum('bkgts,bskd->btkgd', probs, v_heads, preferred_element_type=jn...  55.6 us
    dot_general x2, matrix products, attend(): jnp.einsum('btkgd,bskd->bkgts', q_rot, k_rot, preferred_element_type=jnp....  48.4 us
    reduce_sum x2, other arithmetic, attend(): probs = jax.nn.softmax(scores, axis=-1).astype(jnp.bfloat16)  43.2 us
  transfers between devices with their start and end apart: 14, of which 8 were waited for; matrix products, arithmetic and copies ran while one was open for 32% of the time, Pallas kernels for 0%

commit v1 on v0

--- a/solution.py
+++ b/solution.py
@@ -1,11 +1,164 @@
+import functools
+
 import jax
 import jax.numpy as jnp
 from jax import lax
+from jax.experimental import pallas as pl
+from jax.experimental.pallas import tpu as pltpu
 from jax.sharding import PartitionSpec as P
 
 HEAD = 128
 EPS = 1e-5
 ROPE_BASE = 10000.0
+MESH = pl.DeviceIdType.MESH
+
+LAYERS = 2
+SLOTS = 16
+AHEAD = 4
+AHEAD0 = 2
+
+N_Q = 4
+N_GU = 21
+N_D = 10
+CH_Q = 1
+CH_O = CH_Q + N_Q
+CH_GU = CH_O + N_Q
+CH_GL = CH_GU + N_GU
+CH_D = CH_GL + 1
+CH_DR = CH_D + N_D
+PER_LAYER = CH_DR + 1
+CHUNKS = LAYERS * PER_LAYER
+NAMES = ("q", "k", "v", "o", "g", "u", "d")
+
+
+def gather_kernel(*refs):
+    own = dict(zip(NAMES, refs[:7]))
+    b1 = dict(zip(NAMES, refs[7:14]))
+    b2 = dict(zip(NAMES, refs[14:21]))
+    b3 = dict(zip(NAMES, refs[21:28]))
+    s0s, s0r, s1s, s1r, s2s, s2r, s3s, s3r = refs[28:]
+    y = lax.axis_index("rep")
+    d = lax.axis_index("fsdp")
+    core = lax.rem(d, 2)
+    x_dev = (y, lax.rem(d + 2, 4))
+    y_dev = (1 - y, d)
+    c_dev = (y, d + 1 - 2 * core)
+
+    barrier = pltpu.get_barrier_semaphore()
+    for dev in (x_dev, y_dev, c_dev):
+        pl.semaphore_signal(barrier, inc=1, device_id=dev, device_id_type=MESH)
+    pl.semaphore_wait(barrier, 3)
+
+    def for_chunk(k, fn, lo=0, hi=CHUNKS):
+        layer = k // PER_LAYER
+        i = lax.rem(k, PER_LAYER)
+        slot = lax.rem(k, SLOTS)
+        ok = (k >= lo) & (k < hi)
+
+        def case(cond, items):
+            @pl.when(ok & cond)
+            def _():
+                for n, (name, r0, nr, c0, nc) in enumerate(items):
+                    fn(name, layer, r0, nr, c0, nc, slot, n)
+
+        case(i == 0, [("k", 0, 512, 0, 256), ("v", 0, 512, 0, 256)])
+        jq = pl.multiple_of((i - CH_Q) * 512, 512)
+        case((i >= CH_Q) & (i < CH_O), [("q", 0, 512, jq, 512)])
+        jo = pl.multiple_of((i - CH_O) * 512, 512)
+        case((i >= CH_O) & (i < CH_GU), [("o", 0, 512, jo, 512)])
+        jg = pl.multiple_of((i - CH_GU) * 512, 512)
+        case((i >= CH_GU) & (i < CH_GL), [("g", 0, 512, jg, 512), ("u", 0, 512, jg, 512)])
+        case(i == CH_GL, [("g", 0, 512, N_GU * 512, 256), ("u", 0, 512, N_GU * 512, 256)])
+        jd = core * 192 + (i - CH_D) * 256
+        case((i >= CH_D) & (i < CH_DR), [("d", jd, 256, 0, 2048)])
+        case(i == CH_DR, [("d", (1 - core) * 2560, 192, 0, 2048)])
+
+    def view(bufs, name, layer, r0, nr, c0, nc, half):
+        if half:
+            nr = nr // 2
+            r0 = r0 + y * nr
+        r0 = pl.multiple_of(r0, 32)
+        return bufs[name].at[layer, pl.ds(r0, nr), pl.ds(c0, nc)]
+
+    def copy0(name, layer, r0, nr, c0, nc, slot, n):
+        return pltpu.make_async_remote_copy(
+            src_ref=view(own, name, layer, r0, nr, c0, nc, False),
+            dst_ref=view(b1, name, layer, r0, nr, c0, nc, False),
+            send_sem=s0s.at[slot, n], recv_sem=s0r.at[slot, n], device_id=c_dev, device_id_type=MESH)
+
+    def copy1(name, layer, r0, nr, c0, nc, slot, n):
+        return pltpu.make_async_remote_copy(
+            src_ref=view(own, name, layer, r0, nr, c0, nc, True),
+            dst_ref=view(b2, name, layer, r0, nr, c0, nc, True),
+            send_sem=s1s.at[slot, n], recv_sem=s1r.at[slot, n], device_id=x_dev, device_id_type=MESH)
+
+    def copy2(name, layer, r0, nr, c0, nc, slot, n):
+        return pltpu.make_async_remote_copy(
+            src_ref=view(b2, name, layer, r0, nr, c0, nc, True),
+            dst_ref=view(b2, name, layer, r0, nr, c0, nc, True),
+            send_sem=s2s.at[slot, n], recv_sem=s2r.at[slot, n], device_id=y_dev, device_id_type=MESH)
+
+    def copy3(name, layer, r0, nr, c0, nc, slot, n):
+        return pltpu.make_async_remote_copy(
+            src_ref=view(b2, name, layer, r0, nr, c0, nc, False),
+            dst_ref=view(b3, name, layer, r0, nr, c0, nc, False),
+            send_sem=s3s.at[slot, n], recv_sem=s3r.at[slot, n], device_id=c_dev, device_id_type=MESH)
+
+    def start1(*a):
+        copy1(*a).start()
+
+    def start0(*a):
+        copy0(*a).start()
+
+    def relay2(*a):
+        copy1(*a).wait_recv()
+        copy2(*a).start()
+
+    def relay3(*a):
+        copy2(*a).wait_recv()
+        copy3(*a).start()
+
+    def finish(*a):
+        copy0(*a).wait_recv()
+        copy3(*a).wait_recv()
+        copy0(*a).wait_send()
+        copy1(*a).wait_send()
+        copy2(*a).wait_send()
+        copy3(*a).wait_send()
+
+    def tick(k):
+        for_chunk(k + AHEAD, start1, AHEAD)
+        for_chunk(k + AHEAD0, start0, AHEAD0)
+        for_chunk(k, relay2)
+        for_chunk(k - 1, relay3)
+        for_chunk(k - 2, finish)
+
+    @pl.loop(0, AHEAD)
+    def _(k):
+        for_chunk(k, start1)
+
+    @pl.loop(0, AHEAD0)
+    def _(k):
+        for_chunk(k, start0)
+
+    @pl.loop(0, CHUNKS + 2)
+    def _(k):
+        tick(k)
+
+
+def gather_all(*weights):
+    shapes = [jax.ShapeDtypeStruct(w.shape, w.dtype) for w in weights]
+    sem = pltpu.SemaphoreType.DMA((SLOTS, 2))
+    outs = pl.pallas_call(
+        gather_kernel,
+        out_shape=shapes * 3,
+        in_specs=[pl.BlockSpec(memory_space=pl.ANY)] * 7,
+        out_specs=[pl.BlockSpec(memory_space=pl.ANY)] * 21,
+        scratch_shapes=[sem] * 8,
+        compiler_params=pltpu.CompilerParams(collective_id=0, has_side_effects=True),
+        name="gather_weights",
+    )(*weights)
+    return outs[:7], outs[7:14], outs[14:21]
 
 
 def rms_norm(hidden, gain):
@@ -57,22 +210,19 @@
     return mixed.astype(jnp.bfloat16).reshape(n_blk, n_tok, q_proj.shape[2])
 
 
-def decoder_layer(hidden, allowed, cos_tab, sin_tab, w_q, w_k, w_v, w_o, w_gate, w_up, w_down, g_attn, g_mlp):
+def decoder_layer(hidden, allowed, cos_tab, sin_tab, full, perm, g_attn, g_mlp):
+    def mul(lhs, name):
+        return jnp.dot(perm(lhs), full[name], preferred_element_type=jnp.float32)
+
     normed = rms_norm(hidden, g_attn)
-    q_proj = jnp.dot(normed, w_q, preferred_element_type=jnp.float32).astype(jnp.bfloat16)
-    k_proj = jnp.dot(normed, w_k, preferred_element_type=jnp.float32).astype(jnp.bfloat16)
-    v_proj = jnp.dot(normed, w_v, preferred_element_type=jnp.float32).astype(jnp.bfloat16)
+    q_proj = mul(normed, "q").astype(jnp.bfloat16)
+    k_proj = mul(normed, "k").astype(jnp.bfloat16)
+    v_proj = mul(normed, "v").astype(jnp.bfloat16)
     mixed = attend(q_proj, k_proj, v_proj, allowed, cos_tab, sin_tab)
-    hidden = hidden + jnp.dot(mixed, w_o, preferred_element_type=jnp.float32)
+    hidden = hidden + mul(mixed, "o")
     normed = rms_norm(hidden, g_mlp)
-    gate_proj = jnp.dot(normed, w_gate, preferred_element_type=jnp.float32)
-    up_proj = jnp.dot(normed, w_up, preferred_element_type=jnp.float32)
-    act_val = (jax.nn.silu(gate_proj) * up_proj).astype(jnp.bfloat16)
-    return hidden + jnp.dot(act_val, w_down, preferred_element_type=jnp.float32)
-
-
-def gather_rows(w_shard):
-    return lax.all_gather(w_shard, "fsdp", axis=0, tiled=True)
+    act_val = (jax.nn.silu(mul(normed, "g")) * mul(normed, "u")).astype(jnp.bfloat16)
+    return hidden + mul(act_val, "d")
 
 
 def solution(mesh):
@@ -86,16 +236,20 @@
         seg_blk = seg_ids.reshape(1, n_tok)
         cos_tab, sin_tab = rope_tables(seg_blk)
         allowed = attention_mask(seg_blk)
+        weights = (w_q, w_k, w_v, w_o, w_gate, w_up, w_down)
+        b1, b2, b3 = gather_all(*weights)
+        d = lax.axis_index("fsdp")
+        order = jnp.stack([d, d + 1 - 2 * lax.rem(d, 2), lax.rem(d + 2, 4), 3 - d])
+
+        def perm(lhs):
+            blocks = lhs.reshape(lhs.shape[:-1] + (4, lhs.shape[-1] // 4))
+            return jnp.take(blocks, order, axis=-2).reshape(lhs.shape)
+
         hidden = tokens.astype(jnp.float32).reshape(1, n_tok, width)
-        for layer in range(w_q.shape[0]):
-            full_q = gather_rows(w_q[layer])
-            full_k = gather_rows(w_k[layer])
-            full_v = gather_rows(w_v[layer])
-            full_o = gather_rows(w_o[layer])
-            full_gate = gather_rows(w_gate[layer])
-            full_up = gather_rows(w_up[layer])
-            full_down = gather_rows(w_down[layer])
-            hidden = decoder_layer(hidden, allowed, cos_tab, sin_tab, full_q, full_k, full_v, full_o, full_gate, full_up, full_down, g_attn[layer], g_mlp[layer])
+        for layer in range(LAYERS):
+            full = {n: jnp.concatenate([w[layer], p[layer], q[layer], r[layer]], axis=0)
+                    for n, w, p, q, r in zip(NAMES, weights, b1, b2, b3)}
+            hidden = decoder_layer(hidden, allowed, cos_tab, sin_tab, full, perm, g_attn[layer], g_mlp[layer])
         return hidden.reshape(n_tok, width)
 
     return jax.shard_map(per_device, mesh=mesh, in_specs=(tok_spec, seg_spec, mat_spec, mat_spec, mat_spec, mat_spec, mat_spec, mat_spec, mat_spec, gain_spec, gain_spec), out_specs=tok_spec, check_vma=False)

time: 1980 us -> 2170 us (1.096)
  waiting for transfers between devices: 1260 us -> 0 us
  Pallas kernels: 0 us -> 848 us
  local copies, waits for them, and re-layouts: 88.8 us -> 577 us
  other arithmetic: 64.7 us -> 140 us
  matrix products: 543 us -> 584 us
    all_gather x14 -> x0, waiting for transfers between devices: 1250 us -> none  [gather_rows(): return lax.all_gather(w_shard, 'fsdp', axis=0, tiled=True)]
    pallas_call x0 -> x1, Pallas kernels: none -> 848 us  [gather_all(): pl.pallas_call(gather_kernel, out_shape=shapes * 3, in_specs=[pl.BlockSpe...]
    squeeze x0 -> x17, local copies, waits for them, and re-layouts: none -> 188 us  [the longest x4 68.5 us: per_device(): r[layer]]
    another operation x2 -> x86, local copies, waits for them, and re-layouts: 0.08 us -> 176 us  [the longest x84 176 us: perm(): return jnp.take(blocks, order, axis=-2).reshape(lhs.shape)]
    gather x0 -> x12, local copies, waits for them, and re-layouts: none -> 78.1 us  [perm(): return jnp.take(blocks, order, axis=-2).reshape(lhs.shape)]
    slice x8 -> x1, local copies, waits for them, and re-layouts: 61.1 us -> 0.19 us  [the longest x1 16.1 us: per_device(): full_down = gather_rows(w_down[layer])]
    convert_element_type x1 -> x3, local copies, waits for them, and re-layouts: 6.4 us -> 66.4 us  [the longest x2 60 us: decoder_layer(): (jax.nn.silu(mul(normed, 'g')) * mul(normed, 'u')).astype(jnp.bfloat16)]
    select_n x0 -> x8, other arithmetic: none -> 55.3 us  [perm(): return jnp.take(blocks, order, axis=-2).reshape(lhs.shape)]
  transfers between devices with their start and end apart: 14 -> 0, of which waited for: 8 -> 0; matrix products, arithmetic and copies ran while one was open for 32% -> 0% of each run, Pallas kernels for 0% -> 0%
where the time goes in v1:
time: 2170 us; the launch traced here: 2150 us
  Pallas kernels  848 us (39%)
  matrix products  584 us (27%)
  local copies, waits for them, and re-layouts  577 us (27%)
  other arithmetic  140 us (6%)
    pallas_call x1, Pallas kernels, gather_all(): pl.pallas_call(gather_kernel, out_shape=shapes * 3, in_specs=[pl.BlockSpe...  848 us
    dot_general x14, matrix products, mul(): return jnp.dot(perm(lhs), full[name], preferred_element_type=jnp.float32)  465 us
    another operation x84, local copies, waits for them, and re-layouts, perm(): return jnp.take(blocks, order, axis=-2).reshape(lhs.shape)  176 us
    gather x12, local copies, waits for them, and re-layouts, perm(): return jnp.take(blocks, order, axis=-2).reshape(lhs.shape)  78.1 us
    squeeze x4, local copies, waits for them, and re-layouts, per_device(): r[layer]  68.5 us
    dot_general x2, matrix products, attend(): jnp.einsum('btkgd,bskd->bkgts', q_rot, k_rot, preferred_element_type=jnp....  63.7 us
    squeeze x4, local copies, waits for them, and re-layouts, per_device(): p[layer]  60.5 us
    convert_element_type x2, local copies, waits for them, and re-layouts, decoder_layer(): (jax.nn.silu(mul(normed, 'g')) * mul(normed, 'u')).astype(jnp.bfloat16)  60 us

profile of v1, /device:TPU:0, one launch (start us, length us, event | category | flops | bytes accessed | tf_op | source)
XLA Modules:
  0.0 2151.0 jit_solution(5295644864218653734)
XLA Ops:
  26.4 847.9 %gather_weights.1 = (bf16[2,512,2048]{2,1,0:T(8,128)(2,1)}, bf16[2,512,256]{2,1,0:T(8,128)(2,1)}, bf16[2,512,256]{2,1,0:T(8,128)(2,1)}, bf16[2,512,2048]{2,1,0:T...) custom-call(bf16[2,512,2048]{2,1,0:T(8,128)(2,1)} %refs_0_.1, ...), custom_call_target="tpu_custom_call" | custom-call | tf_op jit(solution)/shard_map/gather_weights/pallas_call | solution.py:152
  926.0 31.6 %fusion.2 = (f32[2,8,1024]{2,1,0:T(8,128)S(1)}, f32[2,1024,1024,8]{2,1,3,0:T(8,128)}) fusion(pred[1024,1024]{0,1:T(8,128)(4,1)S(1)} %fusion.115, bf16[1024,2,8,64]{3,0,2,1:T(8,128)(2,1)} %get-tuple-element.162, bf16[1024,2,8,64]{3,0,2,1:T(8,128)(2,1)} %get-tuple-element.161, bf16[1024,2,64]{2,0,1:T(8,128)(2,1)S(1)} %get-tuple-element.186, ...), kind=kOutput, calls=%fused_computation.28 | convolution fusion | flops 4354719744 | bytes 72941568 | tf_op jit(solution)/shard_map/btkgd,bskd->bkgts/dot_general | solution.py:206
  957.7 21.6 %fusion = f32[2,8,1024]{2,1,0:T(8,128)S(1)} fusion(f32[2,1024,1024,8]{2,1,3,0:T(8,128)} %get-tuple-element.214, f32[2,8,1024]{2,1,0:T(8,128)S(1)} %get-tuple-element.213, pred[1024,1024]{0,1:T(8,128)(4,1)S(1)} %fusion.115), kind=kLoop, calls=%fused_computation.26 | loop fusion | flops 67092480 | bytes 68288512 | tf_op jit(solution)/shard_map/reduce_sum | solution.py:208
  979.3 27.8 %fusion.132 = bf16[2,128,8,1024]{3,1,2,0:T(8,128)(2,1)} fusion(bf16[1024,2,128,1]{0,2,3,1:T(8,128)(2,1)S(1)} %bitcast.392, f32[2,8,1024]{2,1,0:T(8,128)S(1)} %fusion, f32[2,8,1024]{2,1,0:T(8,128)S(1)} %get-tuple-element.213, f32[2,1024,1024,8]{2,1,3,0:T(8,128)} %get-tuple-element.214, pred[1024,1024]{0,1:T(8,128)(4,1)S(1)} %fusion.115), kind=kOutput, calls=%fused_computation.197 | convolution fusion | flops 4380950528 | bytes 73007104 | tf_op jit(solution)/shard_map/bkgts,bskd->btkgd/dot_general | solution.py:209
  1061.2 29.2 %slice_bitcast_fusion.6 = (bf16[512,11008]{1,0:T(8,128)(2,1)}, bf16[512,11008]{1,0:T(8,128)(2,1)}, bf16[512,11008]{1,0:T(8,128)(2,1)}, bf16[512,11008]{1,0:T(8,128)(2,1)}) fusion(bf16[2,512,11008]{2,1,0:T(8,128)(2,1)} %get-tuple-element.43, bf16[2,512,11008]{2,1,0:T(8,128)(2,1)} %get-tuple-element.42), kind=kLoop, calls=%fused_computation.95 | loop fusion | bytes 90177536 | tf_op jit(solution)/shard_map/squeeze | solution.py:250
  1090.4 31.3 %slice_bitcast_fusion.9 = (bf16[512,11008]{1,0:T(8,128)(2,1)}, bf16[512,11008]{1,0:T(8,128)(2,1)}, bf16[512,11008]{1,0:T(8,128)(2,1)}, bf16[512,11008]{1,0:T(8,128)(2,1)}) fusion(bf16[2,512,11008]{2,1,0:T(8,128)(2,1)} %get-tuple-element.41, bf16[2,512,11008]{2,1,0:T(8,128)(2,1)} %get-tuple-element.40), kind=kLoop, calls=%fused_computation.98 | loop fusion | bytes 90177536 | tf_op jit(solution)/shard_map/squeeze | solution.py:250
  1134.3 60.8 %fusion.4 = f32[1024,11008]{1,0:T(8,128)} fusion(bf16[1024,2048]{0,1:T(8,128)(2,1)} %bitcast.374, bf16[512,11008]{1,0:T(8,128)(2,1)} %get-tuple-element.227, bf16[512,11008]{1,0:T(8,128)(2,1)} %get-tuple-element.154, bf16[512,11008]{1,0:T(8,128)(2,1)} %get-tuple-element.229, bf16[512,11008]{1,0:T(8,128)(2,1)} %get-tuple-element.150), kind=kOutput, calls=%fused_computation.30 | convolution fusion | flops 46351253504 | bytes 94371840 | tf_op jit(solution)/shard_map/dot_general | solution.py:215
  1195.1 31.3 %slice_bitcast_fusion.4 = (bf16[512,11008]{1,0:T(8,128)(2,1)}, bf16[512,11008]{1,0:T(8,128)(2,1)}, bf16[512,11008]{1,0:T(8,128)(2,1)}, bf16[512,11008]{1,0:T(8,128)(2,1)}) fusion(bf16[2,512,11008]{2,1,0:T(8,128)(2,1)} %get-tuple-element.45, bf16[2,512,11008]{2,1,0:T(8,128)(2,1)} %get-tuple-element.44), kind=kLoop, calls=%fused_computation.93 | loop fusion | bytes 90177536 | tf_op jit(solution)/shard_map/squeeze | solution.py:250
  1239.0 69.3 %multiply_convert_fusion.1 = bf16[1024,11008]{1,0:T(8,128)(2,1)} fusion(f32[1024,11008]{1,0:T(8,128)} %fusion.4, bf16[1024,2048]{0,1:T(8,128)(2,1)} %bitcast.375, bf16[512,11008]{1,0:T(8,128)(2,1)} %get-tuple-element.148, bf16[512,11008]{1,0:T(8,128)(2,1)} %get-tuple-element.225, bf16[512,11008]{1,0:T(8,128)(2,1)} %get-tuple-element.144, ...), kind=kOutput, calls=%fused_computation.79 | convolution fusion | flops 46418886656 | bytes 116916224 | tf_op jit(solution)/shard_map/dot_general | solution.py:215
  1308.3 30.0 %copy.25 = bf16[1024,11008]{0,1:T(8,128)(2,1)} copy(bf16[1024,11008]{1,0:T(8,128)(2,1)} %multiply_convert_fusion.1) | data formatting | bytes 45088768 | tf_op jit(solution)/shard_map/convert_element_type | solution.py:224
  1366.2 39.3 %while.9 = (s32[]{:T(128)}, bf16[1,1024,4,1024]{1,3,2,0:T(8,128)(2,1)}, s32[4,1]{0,1:T(1,128)S(1)}, bf16[4,1,1024,1024]{2,3,0,1:T(8,128)(2,1)}, s32[]{:T(128)}) while((s32[]{:T(128)}, bf16[1,1024,4,1024]{1,3,2,0:T(8,128)(2,1)}, s32[4,1]{0,1:T(1,128)S(1)}, bf16[4,1,1024,1024]{2,3,0,1:T(8,128)(2,1)}, s32[]{:T(128)}) %tuple.139), condition=%wide.while_cond.1, body=%wide.while_body.1.sunk | while | flops 2 | bytes 16777304 | solution.py:246
  1410.0 39.5 %while.8 = (s32[]{:T(128)}, bf16[1,1024,4,1024]{1,3,2,0:T(8,128)(2,1)}, s32[4,1]{0,1:T(1,128)S(1)}, bf16[4,1,1024,1024]{2,3,0,1:T(8,128)(2,1)}, s32[]{:T(128)}) while((s32[]{:T(128)}, bf16[1,1024,4,1024]{1,3,2,0:T(8,128)(2,1)}, s32[4,1]{0,1:T(1,128)S(1)}, bf16[4,1,1024,1024]{2,3,0,1:T(8,128)(2,1)}, s32[]{:T(128)}) %tuple.140), condition=%wide.while_cond, body=%wide.while_body.sunk | while | flops 2 | bytes 16777304 | solution.py:246
  1466.0 32.1 %slice_bitcast_fusion = (bf16[2752,2048]{1,0:T(8,128)(2,1)}, bf16[2752,2048]{1,0:T(8,128)(2,1)}, bf16[2752,2048]{1,0:T(8,128)(2,1)}, bf16[2752,2048]{1,0:T(8,128)(2,1)}) fusion(bf16[2,2752,2048]{2,1,0:T(8,128)(2,1)} %get-tuple-element.48, bf16[2,2752,2048]{2,1,0:T(8,128)(2,1)} %get-tuple-element.47), kind=kLoop, calls=%fused_computation.89 | loop fusion | bytes 90177536 | tf_op jit(solution)/shard_map/squeeze | solution.py:250
  1501.8 23.3 %slice_bitcast_fusion.2 = (bf16[2752,2048]{1,0:T(8,128)(2,1)}, bf16[2752,2048]{1,0:T(8,128)(2,1)}, bf16[2752,2048]{1,0:T(8,128)(2,1)}, bf16[2752,2048]{1,0:T(8,128)(2,1)}) fusion(bf16[2,2752,2048]{2,1,0:T(8,128)(2,1)} %get-tuple-element.46, bf16[2,2752,2048]{2,1,0:T(8,128)(2,1)S(1)} %bitcast.349), kind=kLoop, calls=%fused_computation.91 | loop fusion | bytes 90177536 | tf_op jit(solution)/shard_map/squeeze | solution.py:250
  1525.1 72.0 %multiply_reduce_fusion.1 = (f32[1024]{0:T(1024)S(1)}, f32[1024,2048]{1,0:T(8,128)}) fusion(f32[1024,2048]{1,0:T(8,128)} %copy-done.9, bf16[1024,11008]{0,1:T(8,128)(2,1)} %bitcast.361, bf16[2752,2048]{1,0:T(8,128)(2,1)} %get-tuple-element.138, bf16[2752,2048]{1,0:T(8,128)(2,1)} %get-tuple-element.223, bf16[2752,2048]{1,0:T(8,128)(2,1)} %get-tuple-element.134, ...), kind=kOutput, calls=%fused_computation.167 | convolution fusion | flops 46357544960 | bytes 84414464 | tf_op jit(solution)/shard_map/dot_general | solution.py:215
  1663.4 32.0 %fusion.3 = (f32[2,8,1024]{2,1,0:T(8,128)S(1)}, f32[2,1024,1024,8]{2,1,3,0:T(8,128)}) fusion(pred[1024,1024]{0,1:T(8,128)(4,1)S(1)} %copy-done.1, bf16[1024,2,8,64]{3,0,2,1:T(8,128)(2,1)} %get-tuple-element.160, bf16[1024,2,8,64]{3,0,2,1:T(8,128)(2,1)} %get-tuple-element.159, bf16[1024,2,64]{2,0,1:T(8,128)(2,1)S(1)} %get-tuple-element.184, ...), kind=kOutput, calls=%fused_computation.29 | convolution fusion | flops 4354719744 | bytes 72941568 | tf_op jit(solution)/shard_map/btkgd,bskd->bkgts/dot_general | solution.py:206
  1695.4 21.6 %fusion.1 = f32[2,8,1024]{2,1,0:T(8,128)S(1)} fusion(f32[2,1024,1024,8]{2,1,3,0:T(8,128)} %get-tuple-element.220, f32[2,8,1024]{2,1,0:T(8,128)S(1)} %get-tuple-element.219, pred[1024,1024]{0,1:T(8,128)(4,1)S(1)} %copy-done.1), kind=kLoop, calls=%fused_computation.27 | loop fusion | flops 67092480 | bytes 68288512 | tf_op jit(solution)/shard_map/reduce_sum | solution.py:208
  1717.1 27.7 %fusion.135 = bf16[2,128,8,1024]{3,1,2,0:T(8,128)(2,1)} fusion(bf16[1024,2,128,1]{0,2,3,1:T(8,128)(2,1)S(1)} %bitcast.393, f32[2,8,1024]{2,1,0:T(8,128)S(1)} %fusion.1, f32[2,8,1024]{2,1,0:T(8,128)S(1)} %get-tuple-element.219, f32[2,1024,1024,8]{2,1,3,0:T(8,128)} %get-tuple-element.220, pred[1024,1024]{0,1:T(8,128)(4,1)S(1)} %copy-done.1), kind=kOutput, calls=%fused_computation.198 | convolution fusion | flops 4380950528 | bytes 73007104 | tf_op jit(solution)/shard_map/bkgts,bskd->btkgd/dot_general | solution.py:209
  1788.1 62.0 %fusion.28 = f32[1024,11008]{1,0:T(8,128)} fusion(bf16[1024,2048]{0,1:T(8,128)(2,1)S(1)} %bitcast.376, bf16[512,11008]{1,0:T(8,128)(2,1)} %get-tuple-element.228, bf16[512,11008]{1,0:T(8,128)(2,1)} %get-tuple-element.153, bf16[512,11008]{1,0:T(8,128)(2,1)} %get-tuple-element.230, bf16[512,11008]{1,0:T(8,128)(2,1)} %get-tuple-element.149), kind=kOutput, calls=%fused_computation.54 | convolution fusion | flops 46351253504 | bytes 94371840 | tf_op jit(solution)/shard_map/dot_general | solution.py:215
  1850.0 69.2 %multiply_convert_fusion = bf16[1024,11008]{1,0:T(8,128)(2,1)} fusion(f32[1024,11008]{1,0:T(8,128)} %fusion.28, bf16[1024,2048]{0,1:T(8,128)(2,1)} %bitcast.377, bf16[512,11008]{1,0:T(8,128)(2,1)} %get-tuple-element.147, bf16[512,11008]{1,0:T(8,128)(2,1)} %get-tuple-element.226, bf16[512,11008]{1,0:T(8,128)(2,1)} %get-tuple-element.143, ...), kind=kOutput, calls=%fused_computation.78 | convolution fusion | flops 46418886656 | bytes 116916224 | tf_op jit(solution)/shard_map/dot_general | solution.py:215
  1919.2 30.0 %copy.38 = bf16[1024,11008]{0,1:T(8,128)(2,1)} copy(bf16[1024,11008]{1,0:T(8,128)(2,1)} %multiply_convert_fusion) | data formatting | bytes 45088768 | tf_op jit(solution)/shard_map/convert_element_type | solution.py:224
  1977.3 39.9 %while.11 = (s32[]{:T(128)}, bf16[1,1024,4,1024]{1,3,2,0:T(8,128)(2,1)}, s32[4,1]{0,1:T(1,128)S(1)}, bf16[4,1,1024,1024]{2,3,0,1:T(8,128)(2,1)}, s32[]{:T(128)}) while((s32[]{:T(128)}, bf16[1,1024,4,1024]{1,3,2,0:T(8,128)(2,1)}, s32[4,1]{0,1:T(1,128)S(1)}, bf16[4,1,1024,1024]{2,3,0,1:T(8,128)(2,1)}, s32[]{:T(128)}) %tuple.141), condition=%wide.while_cond.1.clone, body=%wide.while_body.1.clone.sunk | while | flops 2 | bytes 16777304 | solution.py:246
  2021.6 39.9 %while.10 = (s32[]{:T(128)}, bf16[1,1024,4,1024]{1,3,2,0:T(8,128)(2,1)}, s32[4,1]{0,1:T(1,128)S(1)}, bf16[4,1,1024,1024]{2,3,0,1:T(8,128)(2,1)}, s32[]{:T(128)}) while((s32[]{:T(128)}, bf16[1,1024,4,1024]{1,3,2,0:T(8,128)(2,1)}, s32[4,1]{0,1:T(1,128)S(1)}, bf16[4,1,1024,1024]{2,3,0,1:T(8,128)(2,1)}, s32[]{:T(128)}) %tuple.142), condition=%wide.while_cond.clone, body=%wide.while_body.clone.sunk | while | flops 2 | bytes 16777304 | solution.py:246
  2078.0 72.5 %fusion.121 = f32[1024,2048]{1,0:T(8,128)} fusion(f32[1024,2048]{1,0:T(8,128)} %get-tuple-element.222, bf16[1024,11008]{0,1:T(8,128)(2,1)} %bitcast.362, bf16[2752,2048]{1,0:T(8,128)(2,1)} %get-tuple-element.137, bf16[2752,2048]{1,0:T(8,128)(2,1)} %get-tuple-element.224, bf16[2752,2048]{1,0:T(8,128)(2,1)} %get-tuple-element.133, ...), kind=kOutput, calls=%fused_computation.194 | convolution fusion | flops 46353350656 | bytes 84410368 | tf_op jit(solution)/shard_map/dot_general | solution.py:215
  (311 shorter events, 526.0 us)
Async XLA Ops:
  26.4 852.0 %copy-start.18 = (bf16[2,512,256]{2,1,0:T(8,128)(2,1)S(1)}, bf16[2,512,256]{2,1,0:T(8,128)(2,1)}, u32[]{:S(2)}) copy-start(bf16[2,512,256]{2,1,0:T(8,128)(2,1)} %refs_2_.1) | copy-start | bytes 1572868
  884.0 95.2 %copy-start = (pred[1024,1024]{0,1:T(8,128)(4,1)}, pred[1024,1024]{0,1:T(8,128)(4,1)S(1)}, u32[]{:S(2)}) copy-start(pred[1024,1024]{0,1:T(8,128)(4,1)S(1)} %fusion.115) | copy-start | bytes 3145732
  886.9 38.8 %copy-start.5 = (f32[1024,64]{1,0:T(8,128)}, f32[1024,64]{1,0:T(8,128)S(1)}, u32[]{:S(2)}) copy-start(f32[1024,64]{1,0:T(8,128)S(1)} %get-tuple-element.211) | copy-start | bytes 786436
  886.9 38.8 %copy-start.7 = (f32[1024,64]{1,0:T(8,128)}, f32[1024,64]{1,0:T(8,128)S(1)}, u32[]{:S(2)}) copy-start(f32[1024,64]{1,0:T(8,128)S(1)} %get-tuple-element.212) | copy-start | bytes 786436
  1090.4 31.7 %slice-start.1 = ((s8[22544384]{0:T(1024)(128)(4,1)}), s8[4194304]{0:T(1024)(128)(4,1)S(1)}, s32[]{:S(2)}) async-start(s8[22544384]{0:T(1024)(128)(4,1)} %bitcast.344), calls=%async_computation.1 | async-start | bytes 8388608
  1090.4 33.3 %slice-start.2 = ((s8[22544384]{0:T(1024)(128)(4,1)}), s8[4194304]{0:T(1024)(128)(4,1)S(1)}, s32[]{:S(2)}) async-start(s8[22544384]{0:T(1024)(128)(4,1)} %bitcast.344), calls=%async_computation.2 | async-start | bytes 8388608
  1090.4 34.5 %slice-start.3 = ((s8[22544384]{0:T(1024)(128)(4,1)}), s8[4194304]{0:T(1024)(128)(4,1)S(1)}, s32[]{:S(2)}) async-start(s8[22544384]{0:T(1024)(128)(4,1)} %bitcast.344), calls=%async_computation.3 | async-start | bytes 8388608
  1090.4 35.7 %slice-start.4 = ((s8[22544384]{0:T(1024)(128)(4,1)}), s8[4194304]{0:T(1024)(128)(4,1)S(1)}, s32[]{:S(2)}) async-start(s8[22544384]{0:T(1024)(128)(4,1)} %bitcast.344), calls=%async_computation.4 | async-start | bytes 8388608
  1090.4 36.1 %slice-start.5 = ((s8[22544384]{0:T(1024)(128)(4,1)}), s8[1572864]{0:T(1024)(128)(4,1)S(1)}, s32[]{:S(2)}) async-start(s8[22544384]{0:T(1024)(128)(4,1)} %bitcast.344), calls=%async_computation.5 | async-start | bytes 3145728
  1195.0 31.7 %slice-start.7 = ((s8[22544384]{0:T(1024)(128)(4,1)}), s8[4194304]{0:T(1024)(128)(4,1)S(1)}, s32[]{:S(2)}) async-start(s8[22544384]{0:T(1024)(128)(4,1)} %bitcast.346), calls=%async_computation.7 | async-start | bytes 8388608
  1195.0 33.3 %slice-start.8 = ((s8[22544384]{0:T(1024)(128)(4,1)}), s8[4194304]{0:T(1024)(128)(4,1)S(1)}, s32[]{:S(2)}) async-start(s8[22544384]{0:T(1024)(128)(4,1)} %bitcast.346), calls=%async_computation.8 | async-start | bytes 8388608
  1195.1 34.5 %slice-start.9 = ((s8[22544384]{0:T(1024)(128)(4,1)}), s8[4194304]{0:T(1024)(128)(4,1)S(1)}, s32[]{:S(2)}) async-start(s8[22544384]{0:T(1024)(128)(4,1)} %bitcast.346), calls=%async_computation.9 | async-start | bytes 8388608
  1195.1 35.7 %slice-start.10 = ((s8[22544384]{0:T(1024)(128)(4,1)}), s8[4194304]{0:T(1024)(128)(4,1)S(1)}, s32[]{:S(2)}) async-start(s8[22544384]{0:T(1024)(128)(4,1)} %bitcast.346), calls=%async_computation.10 | async-start | bytes 8388608
  1195.1 36.1 %slice-start.11 = ((s8[22544384]{0:T(1024)(128)(4,1)}), s8[1572864]{0:T(1024)(128)(4,1)S(1)}, s32[]{:S(2)}) async-start(s8[22544384]{0:T(1024)(128)(4,1)} %bitcast.346), calls=%async_computation.11 | async-start | bytes 3145728
  1410.0 39.5 %copy-start.38 = (pred[4]{0:T(512)(128)(4,1)S(1)}, pred[4]{0:T(512)(128)(4,1)}, u32[]{:S(2)}) copy-start(pred[4]{0:T(512)(128)(4,1)} %copy-done.36) | copy-start | bytes 16
  1466.0 32.2 %slice-start.12 = ((s8[22544384]{0:T(1024)(128)(4,1)}), s8[4194304]{0:T(1024)(128)(4,1)S(1)}, s32[]{:S(2)}) async-start(s8[22544384]{0:T(1024)(128)(4,1)} %bitcast.348), calls=%async_computation.12 | async-start | bytes 8388608
  1466.0 32.2 %slice-start.13 = ((s8[22544384]{0:T(1024)(128)(4,1)}), s8[4194304]{0:T(1024)(128)(4,1)S(1)}, s32[]{:S(2)}) async-start(s8[22544384]{0:T(1024)(128)(4,1)} %bitcast.348), calls=%async_computation.13 | async-start | bytes 8388608
  1466.0 32.6 %slice-start.14 = ((s8[22544384]{0:T(1024)(128)(4,1)}), s8[4194304]{0:T(1024)(128)(4,1)S(1)}, s32[]{:S(2)}) async-start(s8[22544384]{0:T(1024)(128)(4,1)} %bitcast.348), calls=%async_computation.14 | async-start | bytes 8388608
  1466.0 34.2 %slice-start.15 = ((s8[22544384]{0:T(1024)(128)(4,1)}), s8[4194304]{0:T(1024)(128)(4,1)S(1)}, s32[]{:S(2)}) async-start(s8[22544384]{0:T(1024)(128)(4,1)} %bitcast.348), calls=%async_computation.15 | async-start | bytes 8388608
  1466.0 35.4 %slice-start.16 = ((s8[22544384]{0:T(1024)(128)(4,1)}), s8[4194304]{0:T(1024)(128)(4,1)S(1)}, s32[]{:S(2)}) async-start(s8[22544384]{0:T(1024)(128)(4,1)} %bitcast.348), calls=%async_computation.16 | async-start | bytes 8388608
  1466.0 35.8 %slice-start.17 = ((s8[22544384]{0:T(1024)(128)(4,1)}), s8[1572864]{0:T(1024)(128)(4,1)S(1)}, s32[]{:S(2)}) async-start(s8[22544384]{0:T(1024)(128)(4,1)} %bitcast.348), calls=%async_computation.17 | async-start | bytes 3145728
  1525.1 72.0 %copy-start.41 = (f32[1,2048]{1,0:T(1,128)S(1)}, f32[1,2048]{1,0:T(1,128)}, u32[]{:S(2)}) copy-start(f32[1,2048]{1,0:T(1,128)} %get-tuple-element.209) | copy-start | bytes 24580
  1788.1 62.0 %copy-start.13 = (bf16[1,1024,4,512]{1,3,2,0:T(8,128)(2,1)}, bf16[1,1024,4,512]{1,3,2,0:T(8,128)(2,1)S(1)}, u32[]{:S(2)}) copy-start(bf16[1,1024,4,512]{1,3,2,0:T(8,128)(2,1)S(1)} %bitcast_select_fusion.2) | copy-start | bytes 12582916
  2021.6 39.9 %copy-start.40 = (pred[4]{0:T(512)(128)(4,1)S(1)}, pred[4]{0:T(512)(128)(4,1)}, u32[]{:S(2)}) copy-start(pred[4]{0:T(512)(128)(4,1)} %copy-done.36) | copy-start | bytes 16
  (45 other events, 384.9 us)

commit v2 on v1

v2 whole, which is shorter than its diff:
```python
import functools

import jax
import jax.numpy as jnp
from jax import lax
from jax.experimental import pallas as pl
from jax.experimental.pallas import tpu as pltpu
from jax.sharding import PartitionSpec as P

D = 2048
FF = 11008
HEADS = 16
HEAD = 128
TOK = 1024
EPS = 1e-5
ROPE_BASE = 10000.0
MESH = pl.DeviceIdType.MESH
F32 = jnp.float32
BF16 = jnp.bfloat16

LAYERS = 2
SLOTS = 16
AHEAD = 4
AHEAD0 = 2
ROWS = D // 4
FF_ROWS = FF // 4
TAIL = 192
NAMES = ("q", "k", "v", "o", "g", "u", "d")

N_Q = 4
N_GU = 21
N_D = 10
CH_Q = 1
CH_O = CH_Q + N_Q
CH_GU = CH_O + N_Q
CH_GL = CH_GU + N_GU
CH_D = CH_GL + 1
CH_DR = CH_D + N_D
PER_LAYER = CH_DR + 1
CHUNKS = LAYERS * PER_LAYER
TICKS = CHUNKS + 2

N_GT = FF // 256
ST_Q = 1
ST_A = ST_Q + N_Q
ST_O = ST_A + HEADS
ST_G = ST_O + 4
ST_D = ST_G + N_GT
ST_T = ST_D + 20
STEPS = ST_T + 2
ALL_STEPS = LAYERS * STEPS

MB = 256
NB = 128
QB = 256


def layer_kernel(*refs):
    tok, cos_ref, sin_ref, first_ref, gain_ref = refs[:5]
    own = dict(zip(NAMES, refs[5:12]))
    out = refs[12]
    b1 = dict(zip(NAMES, refs[13:20]))
    b2 = dict(zip(NAMES, refs[20:27]))
    b3 = dict(zip(NAMES, refs[27:34]))
    x_ref, h_ref, q_ref, kv_ref, a_ref, wbuf, dbuf, wsem, dsem, iosem = refs[34:44]
    s0s, s0r, s1s, s1r, s2s, s2r, s3s, s3r = refs[44:]
    sources = (own, b1, b2, b3)
    y = lax.axis_index("rep")
    d = lax.axis_index("fsdp")
    side = d // 2
    core = lax.rem(d, 2)
    x_dev = (y, lax.rem(d + 2, 4))
    y_dev = (1 - y, d)
    c_dev = (y, d + 1 - 2 * core)

    def rel(block):
        return 2 * lax.rem(block // 2 + side, 2) + lax.rem(block + core, 2)

    load_tok = pltpu.make_async_copy(tok, q_ref, iosem)
    load_tok.start()

    barrier = pltpu.get_barrier_semaphore()
    for dev in (x_dev, y_dev, c_dev):
        pl.semaphore_signal(barrier, inc=1, device_id=dev, device_id_type=MESH)
    pl.semaphore_wait(barrier, 3)

    def for_chunk(k, fn, lo=0):
        layer = k // PER_LAYER
        i = lax.rem(k, PER_LAYER)
        slot = lax.rem(k, SLOTS)
        ok = (k >= lo) & (k < CHUNKS)

        def case(cond, items):
            @pl.when(ok & cond)
            def _():
                for n, (name, r0, nr, c0, nc) in enumerate(items):
                    fn(name, layer, r0, nr, c0, nc, slot, n)

        case(i == 0, [("k", 0, ROWS, 0, 256), ("v", 0, ROWS, 0, 256)])
        jq = pl.multiple_of((i - CH_Q) * 512, 512)
        case((i >= CH_Q) & (i < CH_O), [("q", 0, ROWS, jq, 512)])
        jo = pl.multiple_of((i - CH_O) * 512, 512)
        case((i >= CH_O) & (i < CH_GU), [("o", 0, ROWS, jo, 512)])
        jg = pl.multiple_of((i - CH_GU) * 512, 512)
        case((i >= CH_GU) & (i < CH_GL), [("g", 0, ROWS, jg, 512), ("u", 0, ROWS, jg, 512)])
        case(i == CH_GL, [("g", 0, ROWS, N_GU * 512, 256), ("u", 0, ROWS, N_GU * 512, 256)])
        jd = core * TAIL + (i - CH_D) * 256
        case((i >= CH_D) & (i < CH_DR), [("d", jd, 256, 0, D)])
        case(i == CH_DR, [("d", (1 - core) * 2560, TAIL, 0, D)])

    def view(bufs, name, layer, r0, nr, c0, nc, half):
        if half:
            nr = nr // 2
            r0 = r0 + y * nr
        r0 = pl.multiple_of(r0, 32)
        return bufs[name].at[layer, pl.ds(r0, nr), pl.ds(c0, nc)]

    def remote(src, dst, ss, rs, dev, half):
        def make(name, layer, r0, nr, c0, nc, slot, n):
            return pltpu.make_async_remote_copy(
                src_ref=view(src, name, layer, r0, nr, c0, nc, half),
                dst_ref=view(dst, name, layer, r0, nr, c0, nc, half),
                send_sem=ss.at[slot, n], recv_sem=rs.at[slot, n], device_id=dev, device_id_type=MESH)
        return make

    copy0 = remote(own, b1, s0s, s0r, c_dev, False)
    copy1 = remote(own, b2, s1s, s1r, x_dev, True)
    copy2 = remote(b2, b2, s2s, s2r, y_dev, True)
    copy3 = remote(b2, b3, s3s, s3r, c_dev, False)

    def start0(*a):
        copy0(*a).start()

    def start1(*a):
        copy1(*a).start()

    def relay2(*a):
        copy1(*a).wait_recv()
        copy2(*a).start()

    def relay3(*a):
        copy2(*a).wait_recv()
        copy3(*a).start()

    def finish(*a):
        copy0(*a).wait_recv()
        copy3(*a).wait_recv()
        copy0(*a).wait_send()
        copy1(*a).wait_send()
        copy2(*a).wait_send()
        copy3(*a).wait_send()

    def tick(k):
        for_chunk(k + AHEAD, start1, AHEAD)
        for_chunk(k + AHEAD0, start0, AHEAD0)
        for_chunk(k, relay2)
        for_chunk(k - 1, relay3)
        for_chunk(k - 2, finish)

    def need(s):
        layer = s // STEPS
        i = lax.rem(s, STEPS)
        v = jnp.where(i < ST_A, 3 + i,
            jnp.where(i < ST_O, 7 + (i - ST_A + 1) * 5 // HEADS,
            jnp.where(i < ST_G, 12,
            jnp.where(i < ST_D, 12 + (i - ST_G) // 2,
            jnp.where(i < ST_T, CH_D + 4 + 2 * ((i - ST_D) // 4), CH_DR + 3)))))
        return jnp.minimum(layer * PER_LAYER + v, TICKS)

    def ticks(lo, hi):
        @pl.loop(lo, hi)
        def _(k):
            tick(k)

    def load_tile(s):
        layer = s // STEPS
        i = lax.rem(s, STEPS)
        slot = lax.rem(s, 2)

        def cols(name, c0, nc, w0):
            for r, src in enumerate(sources):
                pltpu.make_async_copy(src[name].at[layer, :, pl.ds(c0, nc)],
                                      wbuf.at[slot, pl.ds(r * ROWS, ROWS), pl.ds(w0, nc)], wsem.at[slot]).start()

        @pl.when(i == 0)
        def _():
            cols("k", 0, 256, 0)
            cols("v", 0, 256, 256)

        @pl.when((i >= ST_Q) & (i < ST_A))
        def _():
            cols("q", pl.multiple_of((i - ST_Q) * 512, 512), 512, 0)

        @pl.when((i >= ST_O) & (i < ST_G))
        def _():
            cols("o", pl.multiple_of((i - ST_O) * 512, 512), 512, 0)

        @pl.when((i >= ST_G) & (i < ST_D))
        def _():
            c0 = pl.multiple_of((i - ST_G) * 256, 256)
            cols("g", c0, 256, 0)
            cols("u", c0, 256, 256)

        for r, src in enumerate(sources):
            src_core = core if r % 2 == 0 else 1 - core

            @pl.when((i >= ST_D) & (i < ST_T) & (lax.rem(i - ST_D, 4) == r))
            def _():
                r0 = pl.multiple_of(src_core * TAIL + (i - ST_D) // 4 * 512, 64)
                pltpu.make_async_copy(src["d"].at[layer, pl.ds(r0, 512), :], dbuf.at[slot], dsem.at[slot]).start()

            @pl.when(i == ST_T + r // 2)
            def _():
                r0 = pl.multiple_of((1 - src_core) * 2560, 512)
                w0 = pl.multiple_of(src_core * TAIL, TAIL)
                pltpu.make_async_copy(src["d"].at[layer, pl.ds(r0, TAIL), :], dbuf.at[slot, pl.ds(w0, TAIL), :],
                                      dsem.at[slot]).start()

    def norm(layer, which):
        @pl.loop(0, TOK // NB)
        def _(m):
            rows = pl.ds(pl.multiple_of(m * NB, NB), NB)
            total = jnp.zeros((NB, 1), F32)
            for b in range(4):
                blk = x_ref[rows, pl.ds(b * ROWS, ROWS)]
                total = total + jnp.sum(blk * blk, axis=1, keepdims=True)
            inv = lax.rsqrt(total * (1.0 / D) + EPS)
            for b in range(4):
                blk = x_ref[rows, pl.ds(b * ROWS, ROWS)]
                gain = gain_ref[which * LAYERS + layer, :, pl.ds(b * ROWS, ROWS)]
                c0 = pl.multiple_of(rel(b) * ROWS, ROWS)
                h_ref[rows, pl.ds(c0, ROWS)] = (blk * inv * gain).astype(BF16)

    def rotate(vals, rows):
        vals = vals.astype(BF16).astype(F32)
        turned = pltpu.roll(vals, HEAD // 2, 1)
        return (vals * cos_ref[rows, :] + turned * sin_ref[rows, :]).astype(BF16)

    def tile_product(slot, finish_rows):
        @pl.loop(0, TOK // MB)
        def _(m):
            rows = pl.ds(pl.multiple_of(m * MB, MB), MB)
            finish_rows(rows, jnp.dot(h_ref[rows, :], wbuf[slot], preferred_element_type=F32))

    def kv_step(slot):
        def fin(rows, acc):
            for b in range(2):
                kv_ref[rows, pl.ds(b * HEAD, HEAD)] = rotate(acc[:, b * HEAD:(b + 1) * HEAD], rows)
            kv_ref[rows, pl.ds(256, 256)] = acc[:, 256:].astype(BF16)
        tile_product(slot, fin)

    def q_step(slot, j):
        def fin(rows, acc):
            for b in range(4):
                c0 = pl.multiple_of(j * 512 + b * HEAD, HEAD)
                q_ref[rows, pl.ds(c0, HEAD)] = rotate(acc[:, b * HEAD:(b + 1) * HEAD], rows)
        tile_product(slot, fin)

    def o_step(slot, j):
        def fin(rows, acc):
            c0 = pl.ds(pl.multiple_of(j * 512, 512), 512)
            x_ref[rows, c0] = x_ref[rows, c0] + acc
        tile_product(slot, fin)

    def g_step(slot, j):
        def fin(rows, acc):
            gate = acc[:, :256]
            up = acc[:, 256:]
            c0 = pl.multiple_of(j * 256, 256)
            a_ref[rows, pl.ds(c0, 256)] = (gate * jax.nn.sigmoid(gate) * up).astype(BF16)
        tile_product(slot, fin)

    def attend(head):
        kv = head // 8
        q0 = pl.multiple_of(head * HEAD, HEAD)
        k0 = pl.multiple_of(kv * HEAD, HEAD)
        v0 = pl.multiple_of(256 + kv * HEAD, HEAD)
        o0 = pl.multiple_of(rel(head // 4) * ROWS + lax.rem(head, 4) * HEAD, HEAD)
        scale = HEAD ** -0.5
        for b in range(TOK // QB):
            keys = (b + 1) * QB
            rows = pl.ds(b * QB, QB)
            scores = lax.dot_general(q_ref[rows, pl.ds(q0, HEAD)], kv_ref[pl.ds(0, keys), pl.ds(k0, HEAD)],
                                     (((1,), (1,)), ((), ())), preferred_element_type=F32)
            key_idx = lax.broadcasted_iota(jnp.int32, (QB, keys), 1)
            row_idx = lax.broadcasted_iota(jnp.int32, (QB, keys), 0) + b * QB
            ok = (key_idx >= first_ref[rows, :]) & (key_idx <= row_idx)
            scores = jnp.where(ok, scores, -1e30)
            top = jnp.max(scores, axis=1, keepdims=True)
            probs = jnp.exp((scores - top) * scale)
            inv = 1.0 / jnp.sum(probs, axis=1, keepdims=True)
            probs = (probs * inv).astype(BF16)
            mixed = jnp.dot(probs, kv_ref[pl.ds(0, keys), pl.ds(v0, HEAD)], preferred_element_type=F32)
            h_ref[rows, pl.ds(o0, HEAD)] = mixed.astype(BF16)

    def d_step(slot, i):
        r = lax.rem(i, 4)
        src_side = lax.rem(side + r // 2, 2)
        src_core = lax.rem(core + r, 2)
        c0 = pl.multiple_of(src_side * (2 * FF_ROWS) + src_core * (FF_ROWS + TAIL) + i // 4 * 512, HEAD)

        @pl.loop(0, TOK // MB)
        def _(m):
            rows = pl.ds(pl.multiple_of(m * MB, MB), MB)
            x_ref[rows, :] = x_ref[rows, :] + jnp.dot(a_ref[rows, pl.ds(c0, 512)], dbuf[slot], preferred_element_type=F32)

    def t_step(slot, i):
        src_side = lax.rem(side + i, 2)
        c0 = pl.multiple_of(src_side * (2 * FF_ROWS) + 2560, HEAD)

        @pl.loop(0, TOK // MB)
        def _(m):
            rows = pl.ds(pl.multiple_of(m * MB, MB), MB)
            x_ref[rows, :] = x_ref[rows, :] + jnp.dot(a_ref[rows, pl.ds(c0, 2 * TAIL)], dbuf[slot, pl.ds(0, 2 * TAIL), :],
                                                      preferred_element_type=F32)

    def wait_w(slot):
        pltpu.make_async_copy(wbuf.at[slot], wbuf.at[slot], wsem.at[slot]).wait()

    def step(s):
        ticks(need(s), need(s + 1))

        @pl.when(s + 1 < ALL_STEPS)
        def _():
            load_tile(s + 1)

        layer = s // STEPS
        i = lax.rem(s, STEPS)
        slot = lax.rem(s, 2)

        @pl.when((i == 0) | (i == ST_G))
        def _():
            norm(layer, jnp.where(i == 0, 0, 1))

        @pl.when((i < ST_A) | ((i >= ST_O) & (i < ST_D)))
        def _():
            wait_w(slot)

        @pl.when(i == 0)
        def _():
            kv_step(slot)

        @pl.when((i >= ST_Q) & (i < ST_A))
        def _():
            q_step(slot, i - ST_Q)

        @pl.when((i >= ST_A) & (i < ST_O))
        def _():
            attend(i - ST_A)

        @pl.when((i >= ST_O) & (i < ST_G))
        def _():
            o_step(slot, i - ST_O)

        @pl.when((i >= ST_G) & (i < ST_D))
        def _():
            g_step(slot, i - ST_G)

        @pl.when((i >= ST_D) & (i < ST_T))
        def _():
            pltpu.make_async_copy(dbuf.at[slot], dbuf.at[slot], dsem.at[slot]).wait()
            d_step(slot, i - ST_D)

        @pl.when(i >= ST_T)
        def _():
            whole = dbuf.at[slot, pl.ds(0, 2 * TAIL), :]
            pltpu.make_async_copy(whole, whole, dsem.at[slot]).wait()
            t_step(slot, i - ST_T)

    @pl.loop(0, AHEAD)
    def _(k):
        for_chunk(k, start1)

    @pl.loop(0, AHEAD0)
    def _(k):
        for_chunk(k, start0)

    load_tok.wait()

    @pl.loop(0, TOK // NB)
    def _(m):
        rows = pl.ds(pl.multiple_of(m * NB, NB), NB)
        x_ref[rows, :] = q_ref[rows, :].astype(F32)

    ticks(0, need(0))
    load_tile(0)

    @pl.loop(0, ALL_STEPS)
    def _(s):
        step(s)

    store = pltpu.make_async_copy(x_ref, out, iosem)
    store.start()
    store.wait()


def run_layers(tokens, cos_tab, sin_tab, first, gains, weights):
    shapes = [jax.ShapeDtypeStruct(w.shape, w.dtype) for w in weights]
    sem = pltpu.SemaphoreType.DMA((SLOTS, 2))
    any_spec = pl.BlockSpec(memory_space=pl.ANY)
    vmem_spec = pl.BlockSpec(memory_space=pltpu.VMEM)
    outs = pl.pallas_call(
        layer_kernel,
        out_shape=[jax.ShapeDtypeStruct((TOK, D), F32)] + shapes * 3,
        in_specs=[any_spec] + [vmem_spec] * 4 + [any_spec] * 7,
        out_specs=[any_spec] * 22,
        scratch_shapes=[
            pltpu.VMEM((TOK, D), F32),
            pltpu.VMEM((TOK, D), BF16),
            pltpu.VMEM((TOK, D), BF16),
            pltpu.VMEM((TOK, 512), BF16),
            pltpu.VMEM((TOK, FF), BF16),
            pltpu.VMEM((2, D, 512), BF16),
            pltpu.VMEM((2, 512, D), BF16),
            pltpu.SemaphoreType.DMA((2,)),
            pltpu.SemaphoreType.DMA((2,)),
            pltpu.SemaphoreType.DMA,
        ] + [sem] * 8,
        compiler_params=pltpu.CompilerParams(collective_id=0, has_side_effects=True, vmem_limit_bytes=66 * 1000 * 1000),
        name="two_layers",
    )(tokens, cos_tab, sin_tab, first, gains, *weights)
    return outs[0]


def rope_tables(seg_ids):
    tok_idx = lax.iota(jnp.int32, TOK)
    is_first = jnp.concatenate([tok_idx[:1] == 0, seg_ids[1:] != seg_ids[:-1]])
    first = lax.cummax(jnp.where(is_first, tok_idx, 0), axis=0)
    tok_pos = (tok_idx - first).astype(F32)
    half_dim = HEAD // 2
    inv_freq = ROPE_BASE ** (-jnp.arange(half_dim, dtype=F32) / half_dim)
    angles = tok_pos[:, None] * inv_freq[None, :]
    cos, sin = jnp.cos(angles), jnp.sin(angles)
    return jnp.concatenate([cos, cos], axis=1), jnp.concatenate([-sin, sin], axis=1), first[:, None]


def solution(mesh):
    tok_spec = P(("rep", "fsdp"), None)
    seg_spec = P(("rep", "fsdp"))
    mat_spec = P(None, "fsdp", None)
    gain_spec = P(None, None)

    def per_device(tokens, seg_ids, w_q, w_k, w_v, w_o, w_gate, w_up, w_down, g_attn, g_mlp):
        cos_tab, sin_tab, first = rope_tables(seg_ids)
        gains = jnp.concatenate([g_attn, g_mlp], axis=0).astype(F32).reshape(2 * LAYERS, 1, D)
        return run_layers(tokens, cos_tab, sin_tab, first, gains, (w_q, w_k, w_v, w_o, w_gate, w_up, w_down))

    return jax.shard_map(per_device, mesh=mesh, in_specs=(tok_spec, seg_spec, mat_spec, mat_spec, mat_spec, mat_spec, mat_spec, mat_spec, mat_spec, gain_spec, gain_spec), out_specs=tok_spec, check_vma=False)
```

time: 2170 us -> 958 us (0.44)
  matrix products: 584 us -> 0 us
  local copies, waits for them, and re-layouts: 577 us -> 11.1 us
  other arithmetic: 140 us -> 5.15 us
  Pallas kernels: 848 us -> 941 us
    dot_general x18 -> x0, matrix products: 584 us -> none  [the longest x14 465 us: mul(): return jnp.dot(perm(lhs), full[name], preferred_element_type=jnp.float32)]
    squeeze x17 -> x0, local copies, waits for them, and re-layouts: 188 us -> none  [the longest x4 68.5 us: per_device(): r[layer]]
    another operation x86 -> x2, local copies, waits for them, and re-layouts: 176 us -> 1.17 us  [the longest x1 1.05 us: rope_tables(): first = lax.cummax(jnp.where(is_first, tok_idx, 0), axis=0)]
    pallas_call x1, Pallas kernels: 848 us -> 941 us  [run_layers(): pl.pallas_call(layer_kernel, out_shape=[jax.ShapeDtypeStruct((TOK, D), F3...]
    gather x12 -> x0, local copies, waits for them, and re-layouts: 78.1 us -> none  [perm(): return jnp.take(blocks, order, axis=-2).reshape(lhs.shape)]
    convert_element_type x3 -> x0, local copies, waits for them, and re-layouts: 66.4 us -> none  [the longest x2 60 us: decoder_layer(): (jax.nn.silu(mul(normed, 'g')) * mul(normed, 'u')).astype(jnp.bfloat16)]
    select_n x9 -> x1, other arithmetic: 55.3 us -> 0.08 us  [rope_tables(): first = lax.cummax(jnp.where(is_first, tok_idx, 0), axis=0)]
    reduce_sum x3 -> x0, other arithmetic: 46.3 us -> none  [the longest x2 43.2 us: attend(): probs = jax.nn.softmax(scores, axis=-1).astype(jnp.bfloat16)]
where the time goes in v2:
time: 958 us; the launch traced here: 957 us
  Pallas kernels  941 us (98%)
  local copies, waits for them, and re-layouts  11.1 us (1%)
    pallas_call x1, Pallas kernels, run_layers(): pl.pallas_call(layer_kernel, out_shape=[jax.ShapeDtypeStruct((TOK, D), F3...  941 us

profile of v2, /device:TPU:0, one launch (start us, length us, event | category | flops | bytes accessed | tf_op | source)
XLA Modules:
  0.0 957.5 jit_solution(18375344699228921889)
XLA Ops:
  0.0 0.8 slice_compare_fusion
  0.9 0.5 slice.16
  2.0 0.1 add_select_fusion
  2.1 0.3 reduce-window.9
  2.4 0.1 slice.19
  2.5 0.1 slice_reduce_fusion
  2.6 0.1 fusion.1
  2.7 0.7 copy.12
  3.4 0.7 copy.13
  4.1 0.6 maximum_convert_fusion.refs_4_
  4.8 1.0 copy.14.refs_3_
  5.8 1.9 fusion
  7.7 1.3 pad_maximum_fusion
  9.0 940.6 %two_layers.1 = (f32[1024,2048]{1,0:T(8,128)}, bf16[2,512,2048]{2,1,0:T(8,128)(2,1)}, bf16[2,512,256]{2,1,0:T(8,128)(2,1)}, bf16[2,512,256]{2,1,0:T(8,128)(2,1)}...) custom-call(bf16[1024,2048]{1,0:T(8,128)(2,1)} %refs_0_.1, ...), custom_call_target="tpu_custom_call" | custom-call | tf_op jit(solution)/shard_map/two_layers/pallas_call | solution.py:402
  949.6 7.9 copy.16
  (3 shorter events, 0.0 us)

commit v3 on v2

--- a/solution.py
+++ b/solution.py
@@ -20,8 +20,10 @@
 
 LAYERS = 2
 SLOTS = 16
-AHEAD = 4
+AHEAD = 8
 AHEAD0 = 2
+LAG3 = 2
+LAGF = 3
 ROWS = D // 4
 FF_ROWS = FF // 4
 TAIL = 192
@@ -38,7 +40,7 @@
 CH_DR = CH_D + N_D
 PER_LAYER = CH_DR + 1
 CHUNKS = LAYERS * PER_LAYER
-TICKS = CHUNKS + 2
+TICKS = CHUNKS + LAGF
 
 N_GT = FF // 256
 ST_Q = 1
@@ -49,6 +51,7 @@
 ST_T = ST_D + 20
 STEPS = ST_T + 2
 ALL_STEPS = LAYERS * STEPS
+FIRST = 1 + LAGF
 
 MB = 256
 NB = 128
@@ -151,21 +154,27 @@
         copy3(*a).wait_send()
 
     def tick(k):
+        for_chunk(k, relay2)
         for_chunk(k + AHEAD, start1, AHEAD)
         for_chunk(k + AHEAD0, start0, AHEAD0)
-        for_chunk(k, relay2)
-        for_chunk(k - 1, relay3)
-        for_chunk(k - 2, finish)
-
-    def need(s):
-        layer = s // STEPS
+        for_chunk(k - LAG3, relay3)
+        for_chunk(k - LAGF, finish)
+
+    def target(s):
         i = lax.rem(s, STEPS)
-        v = jnp.where(i < ST_A, 3 + i,
-            jnp.where(i < ST_O, 7 + (i - ST_A + 1) * 5 // HEADS,
-            jnp.where(i < ST_G, 12,
-            jnp.where(i < ST_D, 12 + (i - ST_G) // 2,
-            jnp.where(i < ST_T, CH_D + 4 + 2 * ((i - ST_D) // 4), CH_DR + 3)))))
-        return jnp.minimum(layer * PER_LAYER + v, TICKS)
+        lead = jnp.where(i < ST_A, jnp.minimum(8, 5 + i),
+               jnp.where(i < 35, 9 + (i - ST_A) // 4,
+               jnp.where(i < ST_D, 16 + (i - 34) // 2,
+               jnp.where(i < 84, 34 + 2 * ((i - ST_D) // 4) + jnp.minimum(1, lax.rem(i - ST_D, 4)), 44 + (i - 84) // 2))))
+        lead = lead + s // STEPS * PER_LAYER
+        i = lax.rem(s + 1, STEPS)
+        data = jnp.where(i < ST_A, i,
+               jnp.where(i < ST_O, 0,
+               jnp.where(i < ST_G, CH_O + i - ST_O,
+               jnp.where(i < ST_D, CH_GU + (i - ST_G) // 2,
+               jnp.where(i < ST_T, CH_D + 1 + 2 * ((i - ST_D) // 4), CH_DR)))))
+        data = data + 1 + LAGF + (s + 1) // STEPS * PER_LAYER
+        return jnp.minimum(jnp.maximum(lead, data), TICKS)
 
     def ticks(lo, hi):
         @pl.loop(lo, hi)
@@ -318,7 +327,7 @@
         pltpu.make_async_copy(wbuf.at[slot], wbuf.at[slot], wsem.at[slot]).wait()
 
     def step(s):
-        ticks(need(s), need(s + 1))
+        ticks(jnp.where(s == 0, FIRST, target(s - 1)), target(s))
 
         @pl.when(s + 1 < ALL_STEPS)
         def _():
@@ -382,7 +391,7 @@
         rows = pl.ds(pl.multiple_of(m * NB, NB), NB)
         x_ref[rows, :] = q_ref[rows, :].astype(F32)
 
-    ticks(0, need(0))
+    ticks(0, FIRST)
     load_tile(0)
 
     @pl.loop(0, ALL_STEPS)

time: 958 us -> 901 us (0.941)
  Pallas kernels: 941 us -> 884 us
    pallas_call x1, Pallas kernels: 941 us -> 884 us  [run_layers(): pl.pallas_call(layer_kernel, out_shape=[jax.ShapeDtypeStruct((TOK, D), F3...]
where the time goes in v3:
time: 901 us
  Pallas kernels  884 us (98%)
  local copies, waits for them, and re-layouts  11.1 us (1%)
    pallas_call x1, Pallas kernels, run_layers(): pl.pallas_call(layer_kernel, out_shape=[jax.ShapeDtypeStruct((TOK, D), F3...  884 us

profile of v3, /device:TPU:0, one launch (start us, length us, event | category | flops | bytes accessed | tf_op | source)
XLA Modules:
  0.0 901.1 jit_solution(15680255432512028364)
XLA Ops:
  0.0 0.8 slice_compare_fusion
  0.9 0.5 slice.16
  2.0 0.1 add_select_fusion
  2.1 0.3 reduce-window.9
  2.4 0.1 slice.19
  2.5 0.1 slice_reduce_fusion
  2.6 0.1 fusion.1
  2.7 0.7 copy.12
  3.4 0.7 copy.13
  4.1 0.6 maximum_convert_fusion.refs_4_
  4.8 1.0 copy.14.refs_3_
  5.8 1.9 fusion
  7.7 1.3 pad_maximum_fusion
  9.0 884.2 %two_layers.1 = (f32[1024,2048]{1,0:T(8,128)}, bf16[2,512,2048]{2,1,0:T(8,128)(2,1)}, bf16[2,512,256]{2,1,0:T(8,128)(2,1)}, bf16[2,512,256]{2,1,0:T(8,128)(2,1)}...) custom-call(bf16[1024,2048]{1,0:T(8,128)(2,1)} %refs_0_.1, ...), custom_call_target="tpu_custom_call" | custom-call | tf_op jit(solution)/shard_map/two_layers/pallas_call | solution.py:411
  893.2 7.9 copy.16
  (3 shorter events, 0.0 us)

commit v4 on v2

--- a/solution.py
+++ b/solution.py
@@ -2,6 +2,7 @@
 
 import jax
 import jax.numpy as jnp
+import numpy as np
 from jax import lax
 from jax.experimental import pallas as pl
 from jax.experimental.pallas import tpu as pltpu
@@ -20,8 +21,10 @@
 
 LAYERS = 2
 SLOTS = 16
-AHEAD = 4
+AHEAD = 8
 AHEAD0 = 2
+LAG3 = 2
+LAGF = 3
 ROWS = D // 4
 FF_ROWS = FF // 4
 TAIL = 192
@@ -38,7 +41,6 @@
 CH_DR = CH_D + N_D
 PER_LAYER = CH_DR + 1
 CHUNKS = LAYERS * PER_LAYER
-TICKS = CHUNKS + 2
 
 N_GT = FF // 256
 ST_Q = 1
@@ -46,9 +48,10 @@
 ST_O = ST_A + HEADS
 ST_G = ST_O + 4
 ST_D = ST_G + N_GT
-ST_T = ST_D + 20
+ST_T = ST_D + 4 * N_D
 STEPS = ST_T + 2
 ALL_STEPS = LAYERS * STEPS
+LATE = 5
 
 MB = 256
 NB = 128
@@ -56,14 +59,15 @@
 
 
 def layer_kernel(*refs):
-    tok, cos_ref, sin_ref, first_ref, gain_ref = refs[:5]
+    tok, seg, freq, g_attn, g_mlp = refs[:5]
     own = dict(zip(NAMES, refs[5:12]))
     out = refs[12]
     b1 = dict(zip(NAMES, refs[13:20]))
     b2 = dict(zip(NAMES, refs[20:27]))
     b3 = dict(zip(NAMES, refs[27:34]))
-    x_ref, h_ref, q_ref, kv_ref, a_ref, wbuf, dbuf, wsem, dsem, iosem = refs[34:44]
-    s0s, s0r, s1s, s1r, s2s, s2r, s3s, s3r = refs[44:]
+    (x_ref, h_ref, q_ref, kv_ref, a_ref, wbuf, dbuf, cos_ref, sin_ref, first_ref, gain_ref,
+     seg_ref, freq_ref, ga_ref, gm_ref, wsem, dsem, iosem, outsem) = refs[34:53]
+    s0s, s0r, s1s, s1r, s2s, s2r, s3s, s3r = refs[53:]
     sources = (own, b1, b2, b3)
     y = lax.axis_index("rep")
     d = lax.axis_index("fsdp")
@@ -76,8 +80,10 @@
     def rel(block):
         return 2 * lax.rem(block // 2 + side, 2) + lax.rem(block + core, 2)
 
-    load_tok = pltpu.make_async_copy(tok, q_ref, iosem)
-    load_tok.start()
+    inputs = [pltpu.make_async_copy(src, dst, iosem.at[n]) for n, (src, dst) in enumerate(
+        ((tok, q_ref), (seg, seg_ref), (freq, freq_ref), (g_attn, ga_ref), (g_mlp, gm_ref)))]
+    for copy in inputs:
+        copy.start()
 
     barrier = pltpu.get_barrier_semaphore()
     for dev in (x_dev, y_dev, c_dev):
@@ -90,11 +96,11 @@
         slot = lax.rem(k, SLOTS)
         ok = (k >= lo) & (k < CHUNKS)
 
-        def case(cond, items):
+        def case(cond, items, direct=False):
             @pl.when(ok & cond)
             def _():
                 for n, (name, r0, nr, c0, nc) in enumerate(items):
-                    fn(name, layer, r0, nr, c0, nc, slot, n)
+                    fn(direct, name, layer, r0, nr, c0, nc, slot, n)
 
         case(i == 0, [("k", 0, ROWS, 0, 256), ("v", 0, ROWS, 0, 256)])
         jq = pl.multiple_of((i - CH_Q) * 512, 512)
@@ -106,7 +112,9 @@
         case(i == CH_GL, [("g", 0, ROWS, N_GU * 512, 256), ("u", 0, ROWS, N_GU * 512, 256)])
         jd = core * TAIL + (i - CH_D) * 256
         case((i >= CH_D) & (i < CH_DR), [("d", jd, 256, 0, D)])
-        case(i == CH_DR, [("d", (1 - core) * 2560, TAIL, 0, D)])
+        last = [("d", (1 - core) * 2560, TAIL, 0, D)]
+        case((i == CH_DR) & (k < CHUNKS - 1), last)
+        case((i == CH_DR) & (k == CHUNKS - 1), last, True)
 
     def view(bufs, name, layer, r0, nr, c0, nc, half):
         if half:
@@ -116,10 +124,11 @@
         return bufs[name].at[layer, pl.ds(r0, nr), pl.ds(c0, nc)]
 
     def remote(src, dst, ss, rs, dev, half):
-        def make(name, layer, r0, nr, c0, nc, slot, n):
+        def make(direct, name, layer, r0, nr, c0, nc, slot, n):
+            part = half and not direct
             return pltpu.make_async_remote_copy(
-                src_ref=view(src, name, layer, r0, nr, c0, nc, half),
-                dst_ref=view(dst, name, layer, r0, nr, c0, nc, half),
+                src_ref=view(src, name, layer, r0, nr, c0, nc, part),
+                dst_ref=view(dst, name, layer, r0, nr, c0, nc, part),
                 send_sem=ss.at[slot, n], recv_sem=rs.at[slot, n], device_id=dev, device_id_type=MESH)
         return make
 
@@ -135,42 +144,62 @@
         copy1(*a).start()
 
     def relay2(*a):
+        copy0(*a).wait_recv()
         copy1(*a).wait_recv()
-        copy2(*a).start()
+        if not a[0]:
+            copy2(*a).start()
 
     def relay3(*a):
-        copy2(*a).wait_recv()
+        if not a[0]:
+            copy2(*a).wait_recv()
         copy3(*a).start()
 
     def finish(*a):
-        copy0(*a).wait_recv()
         copy3(*a).wait_recv()
         copy0(*a).wait_send()
         copy1(*a).wait_send()
-        copy2(*a).wait_send()
+        if not a[0]:
+            copy2(*a).wait_send()
         copy3(*a).wait_send()
 
-    def tick(k):
-        for_chunk(k + AHEAD, start1, AHEAD)
-        for_chunk(k + AHEAD0, start0, AHEAD0)
-        for_chunk(k, relay2)
-        for_chunk(k - 1, relay3)
-        for_chunk(k - 2, finish)
-
-    def need(s):
-        layer = s // STEPS
+    def targets(s):
         i = lax.rem(s, STEPS)
-        v = jnp.where(i < ST_A, 3 + i,
-            jnp.where(i < ST_O, 7 + (i - ST_A + 1) * 5 // HEADS,
-            jnp.where(i < ST_G, 12,
-            jnp.where(i < ST_D, 12 + (i - ST_G) // 2,
-            jnp.where(i < ST_T, CH_D + 4 + 2 * ((i - ST_D) // 4), CH_DR + 3)))))
-        return jnp.minimum(layer * PER_LAYER + v, TICKS)
-
-    def ticks(lo, hi):
-        @pl.loop(lo, hi)
+        lead = jnp.where(i < ST_A, 5 + i,
+               jnp.where(i < ST_D, jnp.maximum(11 + (i - ST_A) // 3, i // 2),
+               jnp.where(i < ST_T, 17 + i // 4, 46)))
+        lead = jnp.minimum(lead + s // STEPS * PER_LAYER, jnp.where(s < ALL_STEPS - LATE, CHUNKS - 1, CHUNKS))
+        i = lax.rem(s + 1, STEPS)
+        base = (s + 1) // STEPS * PER_LAYER
+        part = lax.rem(i - ST_D + STEPS * 4, 4)
+        in_d = (i >= ST_D) & (i < ST_T)
+        chunk = jnp.where(i < ST_A, i,
+                jnp.where(i < ST_O, ST_A - 1,
+                jnp.where(i < ST_G, CH_O + i - ST_O,
+                jnp.where(i < ST_D, CH_GU + (i - ST_G) // 2,
+                jnp.where(i < ST_T, CH_D + (i - ST_D) // 4, CH_DR)))))
+        chunk = jnp.minimum(chunk + base, CHUNKS - 1)
+        need2 = chunk + jnp.where(in_d & (part == 0), 0, 1)
+        need3 = chunk + jnp.where(in_d & (part < 2), 0, 1)
+        needf = chunk + jnp.where((in_d & (part < 3)) | (i == ST_T), 0, 1)
+        tf = jnp.maximum(lead - LAGF, needf)
+        t3 = jnp.maximum(jnp.maximum(lead - LAG3, need3), tf)
+        t2 = jnp.maximum(jnp.maximum(lead, need2), t3)
+        return t2, t3, tf
+
+    def relays(old, new):
+        @pl.loop(old[0], new[0])
         def _(k):
-            tick(k)
+            for_chunk(k, relay2)
+            for_chunk(k + AHEAD, start1, AHEAD)
+            for_chunk(k + AHEAD0, start0, AHEAD0)
+
+        @pl.loop(old[1], new[1])
+        def _(k):
+            for_chunk(k, relay3)
+
+        @pl.loop(old[2], new[2])
+        def _(k):
+            for_chunk(k, finish)
 
     def load_tile(s):
         layer = s // STEPS
@@ -206,8 +235,8 @@
 
             @pl.when((i >= ST_D) & (i < ST_T) & (lax.rem(i - ST_D, 4) == r))
             def _():
-                r0 = pl.multiple_of(src_core * TAIL + (i - ST_D) // 4 * 512, 64)
-                pltpu.make_async_copy(src["d"].at[layer, pl.ds(r0, 512), :], dbuf.at[slot], dsem.at[slot]).start()
+                r0 = pl.multiple_of(src_core * TAIL + (i - ST_D) // 4 * 256, 64)
+                pltpu.make_async_copy(src["d"].at[layer, pl.ds(r0, 256), :], dbuf.at[slot, pl.ds(0, 256), :], dsem.at[slot]).start()
 
             @pl.when(i == ST_T + r // 2)
             def _():
@@ -284,7 +313,8 @@
                                      (((1,), (1,)), ((), ())), preferred_element_type=F32)
             key_idx = lax.broadcasted_iota(jnp.int32, (QB, keys), 1)
             row_idx = lax.broadcasted_iota(jnp.int32, (QB, keys), 0) + b * QB
-            ok = (key_idx >= first_ref[rows, :]) & (key_idx <= row_idx)
+            first = jnp.concatenate([first_ref[rows, :]] * (keys // HEAD), axis=1)
+            ok = (key_idx >= first) & (key_idx <= row_idx)
             scores = jnp.where(ok, scores, -1e30)
             top = jnp.max(scores, axis=1, keepdims=True)
             probs = jnp.exp((scores - top) * scale)
@@ -293,32 +323,34 @@
             mixed = jnp.dot(probs, kv_ref[pl.ds(0, keys), pl.ds(v0, HEAD)], preferred_element_type=F32)
             h_ref[rows, pl.ds(o0, HEAD)] = mixed.astype(BF16)
 
+    def add_product(slot, c0, depth, final):
+        @pl.loop(0, TOK // MB)
+        def _(m):
+            rows = pl.ds(pl.multiple_of(m * MB, MB), MB)
+            x_ref[rows, :] = x_ref[rows, :] + jnp.dot(a_ref[rows, pl.ds(c0, depth)], dbuf[slot, pl.ds(0, depth), :],
+                                                      preferred_element_type=F32)
+
+            @pl.when(final)
+            def _():
+                pltpu.make_async_copy(x_ref.at[rows, :], out.at[rows, :], outsem.at[m]).start()
+
     def d_step(slot, i):
         r = lax.rem(i, 4)
         src_side = lax.rem(side + r // 2, 2)
         src_core = lax.rem(core + r, 2)
-        c0 = pl.multiple_of(src_side * (2 * FF_ROWS) + src_core * (FF_ROWS + TAIL) + i // 4 * 512, HEAD)
-
-        @pl.loop(0, TOK // MB)
-        def _(m):
-            rows = pl.ds(pl.multiple_of(m * MB, MB), MB)
-            x_ref[rows, :] = x_ref[rows, :] + jnp.dot(a_ref[rows, pl.ds(c0, 512)], dbuf[slot], preferred_element_type=F32)
-
-    def t_step(slot, i):
+        c0 = pl.multiple_of(src_side * (2 * FF_ROWS) + src_core * (FF_ROWS + TAIL) + i // 4 * 256, HEAD)
+        add_product(slot, c0, 256, False)
+
+    def t_step(slot, i, final):
         src_side = lax.rem(side + i, 2)
         c0 = pl.multiple_of(src_side * (2 * FF_ROWS) + 2560, HEAD)
-
-        @pl.loop(0, TOK // MB)
-        def _(m):
-            rows = pl.ds(pl.multiple_of(m * MB, MB), MB)
-            x_ref[rows, :] = x_ref[rows, :] + jnp.dot(a_ref[rows, pl.ds(c0, 2 * TAIL)], dbuf[slot, pl.ds(0, 2 * TAIL), :],
-                                                      preferred_element_type=F32)
+        add_product(slot, c0, 2 * TAIL, final)
 
     def wait_w(slot):
         pltpu.make_async_copy(wbuf.at[slot], wbuf.at[slot], wsem.at[slot]).wait()
 
     def step(s):
-        ticks(need(s), need(s + 1))
+        relays(targets(s - 1), targets(s))
 
         @pl.when(s + 1 < ALL_STEPS)
         def _():
@@ -358,14 +390,15 @@
 
         @pl.when((i >= ST_D) & (i < ST_T))
         def _():
-            pltpu.make_async_copy(dbuf.at[slot], dbuf.at[slot], dsem.at[slot]).wait()
+            whole = dbuf.at[slot, pl.ds(0, 256), :]
+            pltpu.make_async_copy(whole, whole, dsem.at[slot]).wait()
             d_step(slot, i - ST_D)
 
         @pl.when(i >= ST_T)
         def _():
             whole = dbuf.at[slot, pl.ds(0, 2 * TAIL), :]
             pltpu.make_async_copy(whole, whole, dsem.at[slot]).wait()
-            t_step(slot, i - ST_T)
+            t_step(slot, i - ST_T, s == ALL_STEPS - 1)
 
     @pl.loop(0, AHEAD)
     def _(k):
@@ -375,34 +408,56 @@
     def _(k):
         for_chunk(k, start0)
 
-    load_tok.wait()
+    for copy in inputs:
+        copy.wait()
+
+    for n, ref in enumerate((ga_ref, gm_ref)):
+        for layer in range(LAYERS):
+            gain_ref[n * LAYERS + layer] = ref[pl.ds(layer, 1), :].astype(F32)
+    ids = seg_ref[...].astype(F32)
+    lane = lax.broadcasted_iota(jnp.int32, (128, HEAD), 1)
+    for b in range(TOK // 128):
+        rows = pl.ds(b * 128, 128)
+        mine = jnp.transpose(jnp.broadcast_to(ids[b:b + 1, :], (128, 128)))
+        before = jnp.zeros((128, 128), F32)
+        for c in range(TOK // 128):
+            before = before + jnp.where(ids[c:c + 1, :] < mine, 1.0, 0.0)
+        first = jnp.sum(before, axis=1, keepdims=True)
+        pos = lax.broadcasted_iota(jnp.int32, (128, 128), 0).astype(F32) + (b * 128.0) - first
+        angles = pos * freq_ref[...]
+        cos_ref[rows, :] = jnp.cos(angles)
+        sin = jnp.sin(angles)
+        sin_ref[rows, :] = jnp.where(lane < HEAD // 2, -sin, sin)
+        first_ref[rows, :] = jnp.broadcast_to(first, (128, 128)).astype(jnp.int32)
 
     @pl.loop(0, TOK // NB)
     def _(m):
         rows = pl.ds(pl.multiple_of(m * NB, NB), NB)
         x_ref[rows, :] = q_ref[rows, :].astype(F32)
 
-    ticks(0, need(0))
+    relays((0, 0, 0), (1, 1, 1))
     load_tile(0)
 
     @pl.loop(0, ALL_STEPS)
     def _(s):
         step(s)
 
-    store = pltpu.make_async_copy(x_ref, out, iosem)
-    store.start()
-    store.wait()
-
-
-def run_layers(tokens, cos_tab, sin_tab, first, gains, weights):
+    for m in range(TOK // MB):
+        rows = pl.ds(m * MB, MB)
+        pltpu.make_async_copy(x_ref.at[rows, :], out.at[rows, :], outsem.at[m]).wait()
+
+
+def run_layers(tokens, seg_ids, g_attn, g_mlp, weights):
     shapes = [jax.ShapeDtypeStruct(w.shape, w.dtype) for w in weights]
+    half_dim = HEAD // 2
+    freq = np.float32(ROPE_BASE) ** (-np.arange(half_dim, dtype=np.float32) / np.float32(half_dim))
+    freq = jnp.asarray(np.concatenate([freq, freq]).reshape(1, HEAD))
     sem = pltpu.SemaphoreType.DMA((SLOTS, 2))
     any_spec = pl.BlockSpec(memory_space=pl.ANY)
-    vmem_spec = pl.BlockSpec(memory_space=pltpu.VMEM)
     outs = pl.pallas_call(
         layer_kernel,
         out_shape=[jax.ShapeDtypeStruct((TOK, D), F32)] + shapes * 3,
-        in_specs=[any_spec] + [vmem_spec] * 4 + [any_spec] * 7,
+        in_specs=[any_spec] * 12,
         out_specs=[any_spec] * 22,
         scratch_shapes=[
             pltpu.VMEM((TOK, D), F32),
@@ -411,27 +466,24 @@
             pltpu.VMEM((TOK, 512), BF16),
             pltpu.VMEM((TOK, FF), BF16),
             pltpu.VMEM((2, D, 512), BF16),
-            pltpu.VMEM((2, 512, D), BF16),
+            pltpu.VMEM((2, 2 * TAIL, D), BF16),
+            pltpu.VMEM((TOK, HEAD), F32),
+            pltpu.VMEM((TOK, HEAD), F32),
+            pltpu.VMEM((TOK, HEAD), jnp.int32),
+            pltpu.VMEM((2 * LAYERS, 1, D), F32),
+            pltpu.VMEM((TOK // 128, 128), jnp.int32),
+            pltpu.VMEM((1, HEAD), F32),
+            pltpu.VMEM((LAYERS, D), BF16),
+            pltpu.VMEM((LAYERS, D), BF16),
             pltpu.SemaphoreType.DMA((2,)),
             pltpu.SemaphoreType.DMA((2,)),
-            pltpu.SemaphoreType.DMA,
+            pltpu.SemaphoreType.DMA((5,)),
+            pltpu.SemaphoreType.DMA((TOK // MB,)),
         ] + [sem] * 8,
         compiler_params=pltpu.CompilerParams(collective_id=0, has_side_effects=True, vmem_limit_bytes=66 * 1000 * 1000),
         name="two_layers",
-    )(tokens, cos_tab, sin_tab, first, gains, *weights)
+    )(tokens, seg_ids.reshape(TOK // 128, 128), freq, g_attn, g_mlp, *weights)
     return outs[0]
-
-
-def rope_tables(seg_ids):
-    tok_idx = lax.iota(jnp.int32, TOK)
-    is_first = jnp.concatenate([tok_idx[:1] == 0, seg_ids[1:] != seg_ids[:-1]])
-    first = lax.cummax(jnp.where(is_first, tok_idx, 0), axis=0)
-    tok_pos = (tok_idx - first).astype(F32)
-    half_dim = HEAD // 2
-    inv_freq = ROPE_BASE ** (-jnp.arange(half_dim, dtype=F32) / half_dim)
-    angles = tok_pos[:, None] * inv_freq[None, :]
-    cos, sin = jnp.cos(angles), jnp.sin(angles)
-    return jnp.concatenate([cos, cos], axis=1), jnp.concatenate([-sin, sin], axis=1), first[:, None]
 
 
 def solution(mesh):
@@ -441,8 +493,6 @@
     gain_spec = P(None, None)
 
     def per_device(tokens, seg_ids, w_q, w_k, w_v, w_o, w_gate, w_up, w_down, g_attn, g_mlp):
-        cos_tab, sin_tab, first = rope_tables(seg_ids)
-        gains = jnp.concatenate([g_attn, g_mlp], axis=0).astype(F32).reshape(2 * LAYERS, 1, D)
-        return run_layers(tokens, cos_tab, sin_tab, first, gains, (w_q, w_k, w_v, w_o, w_gate, w_up, w_down))
+        return run_layers(tokens, seg_ids, g_attn, g_mlp, (w_q, w_k, w_v, w_o, w_gate, w_up, w_down))
 
     return jax.shard_map(per_device, mesh=mesh, in_specs=(tok_spec, seg_spec, mat_spec, mat_spec, mat_spec, mat_spec, mat_spec, mat_spec, mat_spec, gain_spec, gain_spec), out_specs=tok_spec, check_vma=False)

time: 958 us -> 867 us (0.905)
  Pallas kernels: 941 us -> 859 us
    pallas_call x1, Pallas kernels: 941 us -> 859 us  [run_layers(): pl.pallas_call(layer_kernel, out_shape=[jax.ShapeDtypeStruct((TOK, D), F3...]
where the time goes in v4:
time: 867 us
  Pallas kernels  859 us (99%)
    pallas_call x1, Pallas kernels, run_layers(): pl.pallas_call(layer_kernel, out_shape=[jax.ShapeDtypeStruct((TOK, D), F3...  859 us

profile of v4, /device:TPU:0, one launch (start us, length us, event | category | flops | bytes accessed | tf_op | source)
XLA Modules:
  0.0 867.2 jit_solution(9652767007681607053)
XLA Ops:
  0.0 859.3 %two_layers.1 = (f32[1024,2048]{1,0:T(8,128)}, bf16[2,512,2048]{2,1,0:T(8,128)(2,1)}, bf16[2,512,256]{2,1,0:T(8,128)(2,1)}, bf16[2,512,256]{2,1,0:T(8,128)(2,1)}...) custom-call(bf16[1024,2048]{1,0:T(8,128)(2,1)} %refs_0_.1, ...), custom_call_target="tpu_custom_call" | custom-call | tf_op jit(solution)/shard_map/two_layers/pallas_call | solution.py:457
  859.4 7.9 copy.14

commit v5 on v4

--- a/solution.py
+++ b/solution.py
@@ -48,10 +48,11 @@
 ST_O = ST_A + HEADS
 ST_G = ST_O + 4
 ST_D = ST_G + N_GT
-ST_T = ST_D + 4 * N_D
-STEPS = ST_T + 2
-ALL_STEPS = LAYERS * STEPS
-LATE = 5
+ST_T = ST_D + 4 * N_D - 2
+STEPS = ST_D + 4 * N_D + 2
+ALL_STEPS = LAYERS * STEPS - 3
+FIRST = (3, 2, 1)
+FINAL_K = 256 + 256 + 2 * TAIL
 
 MB = 256
 NB = 128
@@ -61,13 +62,13 @@
 def layer_kernel(*refs):
     tok, seg, freq, g_attn, g_mlp = refs[:5]
     own = dict(zip(NAMES, refs[5:12]))
-    out = refs[12]
-    b1 = dict(zip(NAMES, refs[13:20]))
-    b2 = dict(zip(NAMES, refs[20:27]))
-    b3 = dict(zip(NAMES, refs[27:34]))
+    out, last_out = refs[12:14]
+    b1 = dict(zip(NAMES, refs[14:21]))
+    b2 = dict(zip(NAMES, refs[21:28]))
+    b3 = dict(zip(NAMES, refs[28:35]))
     (x_ref, h_ref, q_ref, kv_ref, a_ref, wbuf, dbuf, cos_ref, sin_ref, first_ref, gain_ref,
-     seg_ref, freq_ref, ga_ref, gm_ref, wsem, dsem, iosem, outsem) = refs[34:53]
-    s0s, s0r, s1s, s1r, s2s, s2r, s3s, s3r = refs[53:]
+     seg_ref, freq_ref, ga_ref, gm_ref, wsem, dsem, iosem, outsem, lastsem) = refs[35:55]
+    s0s, s0r, s1s, s1r, s2s, s2r, s3s, s3r = refs[55:]
     sources = (own, b1, b2, b3)
     y = lax.axis_index("rep")
     d = lax.axis_index("fsdp")
@@ -143,8 +144,10 @@
     def start1(*a):
         copy1(*a).start()
 
+    def wait0(*a):
+        copy0(*a).wait_recv()
+
     def relay2(*a):
-        copy0(*a).wait_recv()
         copy1(*a).wait_recv()
         if not a[0]:
             copy2(*a).start()
@@ -165,22 +168,23 @@
     def targets(s):
         i = lax.rem(s, STEPS)
         lead = jnp.where(i < ST_A, 5 + i,
-               jnp.where(i < ST_D, jnp.maximum(11 + (i - ST_A) // 3, i // 2),
-               jnp.where(i < ST_T, 17 + i // 4, 46)))
-        lead = jnp.minimum(lead + s // STEPS * PER_LAYER, jnp.where(s < ALL_STEPS - LATE, CHUNKS - 1, CHUNKS))
-        i = lax.rem(s + 1, STEPS)
-        base = (s + 1) // STEPS * PER_LAYER
-        part = lax.rem(i - ST_D + STEPS * 4, 4)
-        in_d = (i >= ST_D) & (i < ST_T)
-        chunk = jnp.where(i < ST_A, i,
-                jnp.where(i < ST_O, ST_A - 1,
-                jnp.where(i < ST_G, CH_O + i - ST_O,
-                jnp.where(i < ST_D, CH_GU + (i - ST_G) // 2,
-                jnp.where(i < ST_T, CH_D + (i - ST_D) // 4, CH_DR)))))
-        chunk = jnp.minimum(chunk + base, CHUNKS - 1)
-        need2 = chunk + jnp.where(in_d & (part == 0), 0, 1)
-        need3 = chunk + jnp.where(in_d & (part < 2), 0, 1)
-        needf = chunk + jnp.where((in_d & (part < 3)) | (i == ST_T), 0, 1)
+               jnp.where(i < ST_D, jnp.maximum(11 + (i - ST_A) // 3, i // 2 + 1),
+               jnp.where(i < ST_D + 4 * N_D, 17 + i // 4, 46)))
+        lead = jnp.minimum(lead + s // STEPS * PER_LAYER, CHUNKS - 1)
+        nxt = jnp.minimum(s + 1, ALL_STEPS - 1)
+        i = lax.rem(nxt, STEPS)
+        base = nxt // STEPS * PER_LAYER
+        early = jnp.where(i < ST_A, 1 + i,
+                jnp.where(i < ST_O, ST_A,
+                jnp.where(i < ST_G, 1 + CH_O + i - ST_O, 1 + CH_GU + (i - ST_G) // 2)))
+        j = i - ST_D
+        t = CH_D + j // 4
+        p = lax.rem(j + 4 * STEPS, 4)
+        late = i >= ST_D
+        body = i < ST_T
+        need2 = base + jnp.where(late, jnp.where(body, t + jnp.minimum(p, 1), jnp.where(j < 4 * N_D + 1, CH_DR, CH_DR + 1)), early)
+        need3 = base + jnp.where(late, jnp.where(body, t + p // 2, CH_DR - 1 + (j - 4 * N_D + 2 + 1) // 2), early)
+        needf = base + jnp.where(late, jnp.where(body, t + p // 3, CH_DR - 1 + (j - 4 * N_D + 2) // 2 + (j - 4 * N_D + 2) // 3), early)
         tf = jnp.maximum(lead - LAGF, needf)
         t3 = jnp.maximum(jnp.maximum(lead - LAG3, need3), tf)
         t2 = jnp.maximum(jnp.maximum(lead, need2), t3)
@@ -192,6 +196,7 @@
             for_chunk(k, relay2)
             for_chunk(k + AHEAD, start1, AHEAD)
             for_chunk(k + AHEAD0, start0, AHEAD0)
+            for_chunk(k + 1, wait0)
 
         @pl.loop(old[1], new[1])
         def _(k):
@@ -200,6 +205,20 @@
         @pl.loop(old[2], new[2])
         def _(k):
             for_chunk(k, finish)
+
+    def down_step(i):
+        j = i - ST_D
+        own_rest = i == ST_T
+        other_rest = i == STEPS - 1
+        n = jnp.where(i > ST_T, j - 1, j)
+        in_d = (i >= ST_D) & (n < 4 * N_D) & (i != ST_T)
+        return n // 4, lax.rem(n + 4 * STEPS, 4), in_d, own_rest, other_rest
+
+    def rest_col(side_no):
+        return pl.multiple_of(side_no * (2 * FF_ROWS) + 2560, HEAD)
+
+    def tile_col(side_no, core_no, tile):
+        return pl.multiple_of(side_no * (2 * FF_ROWS) + core_no * (FF_ROWS + TAIL) + tile * 256, HEAD)
 
     def load_tile(s):
         layer = s // STEPS
@@ -230,15 +249,16 @@
             cols("g", c0, 256, 0)
             cols("u", c0, 256, 256)
 
+        tile, part, in_d, own_rest, other_rest = down_step(i)
         for r, src in enumerate(sources):
             src_core = core if r % 2 == 0 else 1 - core
 
-            @pl.when((i >= ST_D) & (i < ST_T) & (lax.rem(i - ST_D, 4) == r))
+            @pl.when(in_d & (part == r))
             def _():
-                r0 = pl.multiple_of(src_core * TAIL + (i - ST_D) // 4 * 256, 64)
+                r0 = pl.multiple_of(src_core * TAIL + tile * 256, 64)
                 pltpu.make_async_copy(src["d"].at[layer, pl.ds(r0, 256), :], dbuf.at[slot, pl.ds(0, 256), :], dsem.at[slot]).start()
 
-            @pl.when(i == ST_T + r // 2)
+            @pl.when(own_rest if r < 2 else other_rest)
             def _():
                 r0 = pl.multiple_of((1 - src_core) * 2560, 512)
                 w0 = pl.multiple_of(src_core * TAIL, TAIL)
@@ -334,23 +354,30 @@
             def _():
                 pltpu.make_async_copy(x_ref.at[rows, :], out.at[rows, :], outsem.at[m]).start()
 
-    def d_step(slot, i):
-        r = lax.rem(i, 4)
-        src_side = lax.rem(side + r // 2, 2)
-        src_core = lax.rem(core + r, 2)
-        c0 = pl.multiple_of(src_side * (2 * FF_ROWS) + src_core * (FF_ROWS + TAIL) + i // 4 * 256, HEAD)
-        add_product(slot, c0, 256, False)
-
-    def t_step(slot, i, final):
-        src_side = lax.rem(side + i, 2)
-        c0 = pl.multiple_of(src_side * (2 * FF_ROWS) + 2560, HEAD)
-        add_product(slot, c0, 2 * TAIL, final)
+    def d_step(slot, tile, part):
+        src_side = lax.rem(side + part // 2, 2)
+        src_core = lax.rem(core + part, 2)
+        add_product(slot, tile_col(src_side, src_core, tile), 256, False)
+
+    def t_step(slot, other, final):
+        add_product(slot, rest_col(lax.rem(side + other, 2)), 2 * TAIL, final)
+
+    def last_columns():
+        far = 1 - side
+        pieces = ((tile_col(far, core, N_D - 1), 256), (tile_col(far, 1 - core, N_D - 1), 256), (rest_col(far), 2 * TAIL))
+        c0 = 0
+        copies = []
+        for n, (col, width) in enumerate(pieces):
+            copies.append(pltpu.make_async_copy(a_ref.at[:, pl.ds(col, width)], last_out.at[:, pl.ds(c0, width)], lastsem.at[n]))
+            c0 += width
+        return copies
 
     def wait_w(slot):
         pltpu.make_async_copy(wbuf.at[slot], wbuf.at[slot], wsem.at[slot]).wait()
 
     def step(s):
-        relays(targets(s - 1), targets(s))
+        before = [jnp.where(s == 0, one, two) for one, two in zip(FIRST, targets(s - 1))]
+        relays(before, targets(s))
 
         @pl.when(s + 1 < ALL_STEPS)
         def _():
@@ -388,17 +415,24 @@
         def _():
             g_step(slot, i - ST_G)
 
-        @pl.when((i >= ST_D) & (i < ST_T))
+        tile, part, in_d, own_rest, other_rest = down_step(i)
+
+        @pl.when(in_d)
         def _():
             whole = dbuf.at[slot, pl.ds(0, 256), :]
             pltpu.make_async_copy(whole, whole, dsem.at[slot]).wait()
-            d_step(slot, i - ST_D)
-
-        @pl.when(i >= ST_T)
+            d_step(slot, tile, part)
+
+        @pl.when(own_rest | other_rest)
         def _():
             whole = dbuf.at[slot, pl.ds(0, 2 * TAIL), :]
             pltpu.make_async_copy(whole, whole, dsem.at[slot]).wait()
-            t_step(slot, i - ST_T, s == ALL_STEPS - 1)
+            t_step(slot, jnp.where(own_rest, 0, 1), s == ALL_STEPS - 1)
+
+        @pl.when(s == (LAYERS - 1) * STEPS + ST_D)
+        def _():
+            for copy in last_columns():
+                copy.start()
 
     @pl.loop(0, AHEAD)
     def _(k):
@@ -435,16 +469,52 @@
         rows = pl.ds(pl.multiple_of(m * NB, NB), NB)
         x_ref[rows, :] = q_ref[rows, :].astype(F32)
 
-    relays((0, 0, 0), (1, 1, 1))
+    for_chunk(0, wait0)
+    relays((0, 0, 0), FIRST)
     load_tile(0)
 
     @pl.loop(0, ALL_STEPS)
     def _(s):
         step(s)
 
+    relays(targets(ALL_STEPS - 1), (CHUNKS, CHUNKS, CHUNKS))
+    for copy in last_columns():
+        copy.wait()
     for m in range(TOK // MB):
         rows = pl.ds(m * MB, MB)
         pltpu.make_async_copy(x_ref.at[rows, :], out.at[rows, :], outsem.at[m]).wait()
+
+
+def result_kernel(x_hbm, a_hbm, w2_hbm, w3_hbm, out, x_ref, a_ref, w_ref, wsem, asem, xsem, osem):
+    core = lax.rem(lax.axis_index("fsdp"), 2)
+    w0 = 0
+    for src, src_core in ((w2_hbm, core), (w3_hbm, 1 - core)):
+        r0 = pl.multiple_of(src_core * TAIL + (N_D - 1) * 256, 64)
+        pltpu.make_async_copy(src.at[LAYERS - 1, pl.ds(r0, 256), :], w_ref.at[pl.ds(w0, 256), :], wsem).start()
+        r0 = pl.multiple_of((1 - src_core) * 2560, 512)
+        d0 = pl.multiple_of(512 + src_core * TAIL, 64)
+        pltpu.make_async_copy(src.at[LAYERS - 1, pl.ds(r0, TAIL), :], w_ref.at[pl.ds(d0, TAIL), :], wsem).start()
+        w0 += 256
+
+    def block(src, dst, sem, m):
+        rows = pl.ds(pl.multiple_of(m * MB, MB), MB)
+        return pltpu.make_async_copy(src.at[rows, :], dst.at[rows, :], sem.at[m])
+
+    pltpu.make_async_copy(a_hbm, a_ref, asem).start()
+    for m in range(TOK // MB):
+        block(x_hbm, x_ref, xsem, m).start()
+    pltpu.make_async_copy(w_ref, w_ref, wsem).wait()
+    pltpu.make_async_copy(a_hbm, a_ref, asem).wait()
+
+    @pl.loop(0, TOK // MB)
+    def _(m):
+        rows = pl.ds(pl.multiple_of(m * MB, MB), MB)
+        block(x_hbm, x_ref, xsem, m).wait()
+        x_ref[rows, :] = x_ref[rows, :] + jnp.dot(a_ref[rows, :], w_ref[...], preferred_element_type=F32)
+        block(x_ref, out, osem, m).start()
+
+    for m in range(TOK // MB):
+        block(x_ref, out, osem, m).wait()
 
 
 def run_layers(tokens, seg_ids, g_attn, g_mlp, weights):
@@ -456,9 +526,9 @@
     any_spec = pl.BlockSpec(memory_space=pl.ANY)
     outs = pl.pallas_call(
         layer_kernel,
-        out_shape=[jax.ShapeDtypeStruct((TOK, D), F32)] + shapes * 3,
+        out_shape=[jax.ShapeDtypeStruct((TOK, D), F32), jax.ShapeDtypeStruct((TOK, FINAL_K), BF16)] + shapes * 3,
         in_specs=[any_spec] * 12,
-        out_specs=[any_spec] * 22,
+        out_specs=[any_spec] * 23,
         scratch_shapes=[
             pltpu.VMEM((TOK, D), F32),
             pltpu.VMEM((TOK, D), BF16),
@@ -479,11 +549,28 @@
             pltpu.SemaphoreType.DMA((2,)),
             pltpu.SemaphoreType.DMA((5,)),
             pltpu.SemaphoreType.DMA((TOK // MB,)),
+            pltpu.SemaphoreType.DMA((3,)),
         ] + [sem] * 8,
         compiler_params=pltpu.CompilerParams(collective_id=0, has_side_effects=True, vmem_limit_bytes=66 * 1000 * 1000),
         name="two_layers",
     )(tokens, seg_ids.reshape(TOK // 128, 128), freq, g_attn, g_mlp, *weights)
-    return outs[0]
+    return pl.pallas_call(
+        result_kernel,
+        out_shape=jax.ShapeDtypeStruct((TOK, D), F32),
+        in_specs=[any_spec] * 4,
+        out_specs=any_spec,
+        scratch_shapes=[
+            pltpu.VMEM((TOK, D), F32),
+            pltpu.VMEM((TOK, FINAL_K), BF16),
+            pltpu.VMEM((FINAL_K, D), BF16),
+            pltpu.SemaphoreType.DMA,
+            pltpu.SemaphoreType.DMA,
+            pltpu.SemaphoreType.DMA((TOK // MB,)),
+            pltpu.SemaphoreType.DMA((TOK // MB,)),
+        ],
+        compiler_params=pltpu.CompilerParams(vmem_limit_bytes=60 * 1000 * 1000),
+        name="result",
+    )(outs[0], outs[1], outs[15], outs[22])
 
 
 def solution(mesh):

time: 867 us -> 865 us (level)
    pallas_call x0 -> x1, Pallas kernels: none -> 10.9 us  [run_layers(): pl.pallas_call(result_kernel, out_shape=jax.ShapeDtypeStruct((TOK, D), F3...]
where the time goes in v5:
time: 865 us
  Pallas kernels  865 us (100%)
    pallas_call x1, Pallas kernels, run_layers(): pl.pallas_call(layer_kernel, out_shape=[jax.ShapeDtypeStruct((TOK, D), F3...  854 us

profile of v5, /device:TPU:0, one launch (start us, length us, event | category | flops | bytes accessed | tf_op | source)
XLA Modules:
  0.0 865.2 jit_solution(1345903586367180349)
XLA Ops:
  0.0 854.3 %two_layers.1 = (f32[1024,2048]{1,0:T(8,128)}, bf16[1024,896]{1,0:T(8,128)(2,1)}, bf16[2,512,2048]{2,1,0:T(8,128)(2,1)}, bf16[2,512,256]{2,1,0:T(8,128)(2,1)}, b...) custom-call(bf16[1024,2048]{1,0:T(8,128)(2,1)} %refs_0_.1, ...), custom_call_target="tpu_custom_call" | custom-call | tf_op jit(solution)/shard_map/two_layers/pallas_call | solution.py:527
  854.3 10.9 %result.1 = f32[1024,2048]{1,0:T(8,128)} custom-call(f32[1024,2048]{1,0:T(8,128)} %get-tuple-element.9.x_hbm, bf16[1024,896]{1,0:T(8,128)(2,1)} %get-tuple-element.10.a_hbm, bf16[2,2752,2048]{2,1,0:T(8,128)(2,1)} %get-tuple-element.11.w2_hbm, bf16[2,2752,2048]{2,1,0:T(8,128)(2,1)} %get-tuple-element.12.w3_hbm), custom_call_target="tpu_custom_call" | custom-call | tf_op jit(solution)/shard_map/result/pallas_call | solution.py:557
